TPU v7x, 16 devices: a whole 2x2x2 slice. The times are simulated.
16 devices in a mesh: dp: 2 (over z), fsdp: 8 (over y, x, core).
Axes of the slice: x: 2, y: 2, z: 2, core: 2. Of those that a mesh axis runs over, the one named last changes fastest.
Arguments:
- tokens: bfloat16 [32, 256, 2048], P(('dp', 'fsdp')), parts along dimension 0
- w_query: bfloat16 [2, 2048, 2048], P(None, 'fsdp')
- w_key: bfloat16 [2, 2048, 2048], P(None, 'fsdp')
- w_value: bfloat16 [2, 2048, 2048], P(None, 'fsdp')
- w_out: bfloat16 [2, 2048, 2048], P(None, 'fsdp')
- w_gate: bfloat16 [2, 2048, 8192], P(None, 'fsdp')
- w_up: bfloat16 [2, 2048, 8192], P(None, 'fsdp')
- w_down: bfloat16 [2, 8192, 2048], P(None, 'fsdp')
- g_query: bfloat16 [2, 2048], P(None, 'fsdp')
- g_key: bfloat16 [2, 2048], P(None, 'fsdp')
- g_attn: bfloat16 [2, 2048], P(None, 'fsdp')
- g_mlp: bfloat16 [2, 2048], P(None, 'fsdp')
Outputs:
- output: bfloat16 [32, 256, 2048], P(('dp', 'fsdp')), parts along dimension 0
There are 2 independent parts. A program takes and returns all parts, laid end to end along the dimension named above; an argument that names none is the same for every part.
All inputs are finite; a program needn't handle non-finite values.
Results may differ from a plain program's by a relative error of at most 0.02.
Values are sent between devices in bfloat16 or wider.
A program may use at most 1 GiB of HBM per device.

v0:
```python
import jax
import jax.numpy as jnp
from jax import lax
from jax.sharding import PartitionSpec as P

HEAD_DIM = 128
EPS = 1e-6
THETA = 500000.0
Q_BLOCK = 256


def rms_norm(values, gain_vec):
    mean_sq = jnp.mean(values * values, axis=-1, keepdims=True)
    return values * lax.rsqrt(mean_sq + EPS) * gain_vec.astype(jnp.float32)


def rope_tables(seq_len):
    positions = jnp.arange(seq_len, dtype=jnp.float32)
    inv_freq = THETA ** (-2.0 * jnp.arange(HEAD_DIM // 2, dtype=jnp.float32) / HEAD_DIM)
    angles = positions[:, None] * inv_freq[None, :]
    return jnp.cos(angles), jnp.sin(angles)


def apply_rope(values, cos_tab, sin_tab):
    half_dim = values.shape[-1] // 2
    first = values[..., :half_dim]
    second = values[..., half_dim:]
    cos_b = cos_tab[:, None, :]
    sin_b = sin_tab[:, None, :]
    return jnp.concatenate([first * cos_b - second * sin_b, second * cos_b + first * sin_b], axis=-1)


def dot_bf16(left, right):
    return jnp.dot(left, right, preferred_element_type=jnp.float32).astype(jnp.bfloat16)


def causal_attention(q_rot, k_rot, v_heads):
    seq_len = q_rot.shape[1]
    q_block = min(seq_len, Q_BLOCK)
    att_scale = HEAD_DIM ** -0.5
    pieces = []
    for block_idx in range(seq_len // q_block):
        start = block_idx * q_block
        stop = start + q_block
        scores = jnp.einsum('bqhd,bkhd->bhqk', q_rot[:, start:stop], k_rot[:, :stop], preferred_element_type=jnp.float32) * att_scale
        q_pos = start + jnp.arange(q_block)
        causal = q_pos[:, None] >= jnp.arange(stop)[None, :]
        scores = jnp.where(causal, scores, -jnp.inf)
        probs = jax.nn.softmax(scores, axis=-1).astype(jnp.bfloat16)
        pieces.append(jnp.einsum('bhqk,bkhd->bqhd', probs, v_heads[:, :stop], preferred_element_type=jnp.float32).astype(jnp.bfloat16))
    return jnp.concatenate(pieces, axis=1)


def layer_forward(x_loc, layer_w, cos_tab, sin_tab):
    w_query, w_key, w_value, w_out, w_gate, w_up, w_down, g_query, g_key, g_attn, g_mlp = layer_w
    n_batch, seq_len, width = x_loc.shape
    n_heads = width // HEAD_DIM
    flat_x = x_loc.reshape(n_batch * seq_len, width)

    def norm_rope(lin_vals, gain_vec):
        normed = rms_norm(lin_vals.astype(jnp.float32), gain_vec).reshape(n_batch, seq_len, n_heads, HEAD_DIM)
        return apply_rope(normed, cos_tab, sin_tab).astype(jnp.bfloat16)

    q_rot = norm_rope(dot_bf16(flat_x, w_query), g_query)
    k_rot = norm_rope(dot_bf16(flat_x, w_key), g_key)
    v_heads = dot_bf16(flat_x, w_value).reshape(n_batch, seq_len, n_heads, HEAD_DIM)
    attn_out = causal_attention(q_rot, k_rot, v_heads).reshape(n_batch * seq_len, width)
    a_lin = dot_bf16(attn_out, w_out)
    hidden = (flat_x.astype(jnp.float32) + rms_norm(a_lin.astype(jnp.float32), g_attn)).astype(jnp.bfloat16)
    gate_proj = dot_bf16(hidden, w_gate)
    up_proj = dot_bf16(hidden, w_up)
    gated = (jax.nn.silu(gate_proj.astype(jnp.float32)) * up_proj.astype(jnp.float32)).astype(jnp.bfloat16)
    down_proj = dot_bf16(gated, w_down)
    result = (hidden.astype(jnp.float32) + rms_norm(down_proj.astype(jnp.float32), g_mlp)).astype(jnp.bfloat16)
    return result.reshape(n_batch, seq_len, width)


def solution(mesh):
    def gather_rows(arr_w, layer_idx):
        return lax.all_gather(arr_w[layer_idx], 'fsdp', axis=0, tiled=True)

    def local_fn(tokens, weights):
        cos_tab, sin_tab = rope_tables(tokens.shape[1])
        current = tokens
        for layer_idx in range(weights[0].shape[0]):
            layer_w = tuple(gather_rows(arr_w, layer_idx) for arr_w in weights)
            current = layer_forward(current, layer_w, cos_tab, sin_tab)
        return current

    mapped = jax.shard_map(local_fn, mesh=mesh, in_specs=(P(('dp', 'fsdp')), P(None, 'fsdp')), out_specs=P(('dp', 'fsdp')), check_vma=False)

    def run(tokens, w_query, w_key, w_value, w_out, w_gate, w_up, w_down, g_query, g_key, g_attn, g_mlp):
        return mapped(tokens, (w_query, w_key, w_value, w_out, w_gate, w_up, w_down, g_query, g_key, g_attn, g_mlp))

    return run
```

profile of v0, /device:TPU:0, one launch (start us, length us, event | category | flops | bytes accessed | tf_op | source)
XLA Modules:
  0.0 1413.7 jit_solution(4187298922869379203)
XLA Ops:
  39.4 10.7 all-gather.2
  50.1 8.9 all-gather.4
  66.9 8.9 all-gather.10
  76.3 7.9 all-gather.13
  84.9 8.8 all-gather.15
  102.9 9.4 all-gather.21
  113.5 8.3 fusion.58
  125.2 8.2 fusion.61
  136.9 30.8 %all-gather.37.cloned.1.call-done = bf16[1,2048,2048]{2,1,0:T(8,128)(2,1)} async-done(((bf16[1,256,2048]{2,1,0:T(8,128)(2,1)}), bf16[1,2048,2048]{2,1,0:T(8,128)(2,1)}) %all-gather.37.cloned.1.call-update) | async-done | bytes 8388624 | tf_op jit(solution)/shard_map/all_gather | solution.py:80
  167.7 8.2 fusion.163
  201.0 18.6 %all-gather.43.cloned.1.call-done = bf16[1,2048,2048]{2,1,0:T(8,128)(2,1)} async-done(((bf16[1,256,2048]{2,1,0:T(8,128)(2,1)}), bf16[1,2048,2048]{2,1,0:T(8,128)(2,1)}) %all-gather.43.cloned.1.call-update) | async-done | bytes 8388624 | tf_op jit(solution)/shard_map/all_gather | solution.py:80
  219.6 8.4 fusion.64
  229.2 149.1 %all-gather.45.cloned.1.call-done = bf16[1,2048,8192]{2,1,0:T(8,128)(2,1)} async-done(((bf16[1,256,8192]{2,1,0:T(8,128)(2,1)}), bf16[1,2048,8192]{2,1,0:T(8,128)(2,1)}) %all-gather.45.cloned.1.call-update) | async-done | bytes 33554448 | tf_op jit(solution)/shard_map/all_gather | solution.py:80
  378.3 25.6 %fusion.24 = bf16[512,8192]{1,0:T(8,128)(2,1)} fusion(bf16[512,2048]{1,0:T(8,128)(2,1)S(1)} %fusion.67, bf16[1,2048,8192]{2,1,0:T(8,128)(2,1)} %all-gather.45.cloned.1.call-done), kind=kOutput, calls=%fused_computation.28 | convolution fusion | flops 17184063488 | bytes 44040192 | tf_op jit(solution)/shard_map/dot_general | solution.py:34
  404.0 133.1 %all-gather.47.cloned.1.call-done = bf16[1,2048,8192]{2,1,0:T(8,128)(2,1)} async-done(((bf16[1,256,8192]{2,1,0:T(8,128)(2,1)}), bf16[1,2048,8192]{2,1,0:T(8,128)(2,1)}) %all-gather.47.cloned.1.call-update) | async-done | bytes 33554448 | tf_op jit(solution)/shard_map/all_gather | solution.py:80
  537.1 25.6 %fusion.122.clone.4 = bf16[512,8192]{1,0:T(8,128)(2,1)} fusion(bf16[512,8192]{1,0:T(8,128)(2,1)} %fusion.24, bf16[512,2048]{1,0:T(8,128)(2,1)S(1)} %fusion.67, bf16[1,2048,8192]{2,1,0:T(8,128)(2,1)} %all-gather.47.cloned.1.call-done), kind=kOutput, calls=%fused_computation.27.clone.clone.clone.clone.clone.clone.1 | convolution fusion | flops 17217617920 | bytes 52428800 | tf_op jit(solution)/shard_map/dot_general | solution.py:34
  562.7 133.3 %all-gather.49.cloned.1.call-done = bf16[1,8192,2048]{2,1,0:T(8,128)(2,1)} async-done(((bf16[1,1024,2048]{2,1,0:T(8,128)(2,1)}), bf16[1,8192,2048]{2,1,0:T(8,128)(2,1)}) %all-gather.49.cloned.1.call-update) | async-done | bytes 33554448 | tf_op jit(solution)/shard_map/all_gather | solution.py:80
  696.0 24.6 %fusion.68 = (f32[512]{0:T(512)S(1)}, bf16[512,2048]{1,0:T(8,128)(2,1)S(1)}) fusion(bf16[1,8192,2048]{2,1,0:T(8,128)(2,1)} %all-gather.49.cloned.1.call-done, bf16[512,8192]{1,0:T(8,128)(2,1)} %fusion.122.clone.4), kind=kOutput, calls=%fused_computation.84 | convolution fusion | flops 17184063488 | bytes 44042240 | tf_op jit(solution)/shard_map/dot_general | solution.py:34
  721.9 26.1 %all-gather.53.cloned.1.call-done = bf16[1,2048,2048]{2,1,0:T(8,128)(2,1)} async-done(((bf16[1,256,2048]{2,1,0:T(8,128)(2,1)}), bf16[1,2048,2048]{2,1,0:T(8,128)(2,1)}) %all-gather.53.cloned.1.call-update) | async-done | bytes 8388624 | tf_op jit(solution)/shard_map/all_gather | solution.py:80
  748.0 8.2 fusion.72
  759.8 40.3 %all-gather.55.cloned.1.call-done = bf16[1,2048,2048]{2,1,0:T(8,128)(2,1)} async-done(((bf16[1,256,2048]{2,1,0:T(8,128)(2,1)}), bf16[1,2048,2048]{2,1,0:T(8,128)(2,1)}) %all-gather.55.cloned.1.call-update) | async-done | bytes 8388624 | tf_op jit(solution)/shard_map/all_gather | solution.py:80
  800.0 8.2 fusion.75
  811.7 40.2 %all-gather.51.cloned.1.call-done = bf16[1,2048,2048]{2,1,0:T(8,128)(2,1)} async-done(((bf16[1,256,2048]{2,1,0:T(8,128)(2,1)}), bf16[1,2048,2048]{2,1,0:T(8,128)(2,1)}) %all-gather.51.cloned.1.call-update) | async-done | bytes 8388624 | tf_op jit(solution)/shard_map/all_gather | solution.py:80
  851.9 8.2 fusion.160
  882.9 21.1 %all-gather.57.cloned.1.call-done = bf16[1,2048,2048]{2,1,0:T(8,128)(2,1)} async-done(((bf16[1,256,2048]{2,1,0:T(8,128)(2,1)}), bf16[1,2048,2048]{2,1,0:T(8,128)(2,1)}) %all-gather.57.cloned.1.call-update) | async-done | bytes 8388624 | tf_op jit(solution)/shard_map/all_gather | solution.py:80
  903.9 8.6 fusion.78
  913.7 149.0 %all-gather.59.cloned.1.call-done = bf16[1,2048,8192]{2,1,0:T(8,128)(2,1)} async-done(((bf16[1,256,8192]{2,1,0:T(8,128)(2,1)}), bf16[1,2048,8192]{2,1,0:T(8,128)(2,1)}) %all-gather.59.cloned.1.call-update) | async-done | bytes 33554448 | tf_op jit(solution)/shard_map/all_gather | solution.py:80
  1062.7 25.5 %fusion.30 = bf16[512,8192]{1,0:T(8,128)(2,1)} fusion(bf16[512,2048]{1,0:T(8,128)(2,1)S(1)} %fusion.81, bf16[1,2048,8192]{2,1,0:T(8,128)(2,1)} %all-gather.59.cloned.1.call-done), kind=kOutput, calls=%fused_computation.30 | convolution fusion | flops 17184063488 | bytes 44040192 | tf_op jit(solution)/shard_map/dot_general | solution.py:34
  1088.2 133.4 %all-gather.61.cloned.1.call-done = bf16[1,2048,8192]{2,1,0:T(8,128)(2,1)} async-done(((bf16[1,256,8192]{2,1,0:T(8,128)(2,1)}), bf16[1,2048,8192]{2,1,0:T(8,128)(2,1)}) %all-gather.61.cloned.1.call-update) | async-done | bytes 33554448 | tf_op jit(solution)/shard_map/all_gather | solution.py:80
  1221.6 25.9 %fusion.131.clone.2 = bf16[512,8192]{1,0:T(8,128)(2,1)} fusion(bf16[512,8192]{1,0:T(8,128)(2,1)} %fusion.30, bf16[512,2048]{1,0:T(8,128)(2,1)S(1)} %fusion.81, bf16[1,2048,8192]{2,1,0:T(8,128)(2,1)} %all-gather.61.cloned.1.call-done), kind=kOutput, calls=%fused_computation.26.clone.clone.clone.clone.clone.clone | convolution fusion | flops 17217617920 | bytes 52428800 | tf_op jit(solution)/shard_map/dot_general | solution.py:34
  1247.5 132.8 %all-gather.63.cloned.1.call-done = bf16[1,8192,2048]{2,1,0:T(8,128)(2,1)} async-done(((bf16[1,1024,2048]{2,1,0:T(8,128)(2,1)}), bf16[1,8192,2048]{2,1,0:T(8,128)(2,1)}) %all-gather.63.cloned.1.call-update) | async-done | bytes 33554448 | tf_op jit(solution)/shard_map/all_gather | solution.py:80
  1380.4 24.1 %fusion.82 = (f32[512]{0:T(512)S(1)}, bf16[512,2048]{1,0:T(8,128)(2,1)S(1)}) fusion(bf16[1,8192,2048]{2,1,0:T(8,128)(2,1)} %all-gather.63.cloned.1.call-done, bf16[512,8192]{1,0:T(8,128)(2,1)} %fusion.131.clone.2), kind=kOutput, calls=%fused_computation.98 | convolution fusion | flops 17184063488 | bytes 44042240 | tf_op jit(solution)/shard_map/dot_general | solution.py:34
  (147 shorter events, 119.2 us)
Async XLA Ops:
  6.5 106.9 %all-gather.39.cloned.1.call-start = ((), (), s32[]{:S(2)}) async-start(), calls=%async_computation.1 | async-start | bytes 9437184 | tf_op jit(solution)/shard_map/all_gather | solution.py:80
  9.9 115.3 %all-gather.41.cloned.1.call-start = ((), (), s32[]{:S(2)}) async-start(), calls=%async_computation.2 | async-start | bytes 9437184 | tf_op jit(solution)/shard_map/all_gather | solution.py:80
  11.4 156.3 %all-gather.37.cloned.1.call-start = ((), (), s32[]{:S(2)}) async-start(), calls=%async_computation | async-start | bytes 9437184 | tf_op jit(solution)/shard_map/all_gather | solution.py:80
  14.8 204.8 %all-gather.43.cloned.1.call-start = ((), (), s32[]{:S(2)}) async-start(), calls=%async_computation.3 | async-start | bytes 9437184 | tf_op jit(solution)/shard_map/all_gather | solution.py:80
  16.3 362.0 %all-gather.45.cloned.1.call-start = ((), (), s32[]{:S(2)}) async-start(), calls=%async_computation.4 | async-start | bytes 37748736 | tf_op jit(solution)/shard_map/all_gather | solution.py:80
  22.4 514.6 %all-gather.47.cloned.1.call-start = ((), (), s32[]{:S(2)}) async-start(), calls=%async_computation.5 | async-start | bytes 37748736 | tf_op jit(solution)/shard_map/all_gather | solution.py:80
  28.5 667.5 %all-gather.49.cloned.1.call-start = ((), (), s32[]{:S(2)}) async-start(), calls=%async_computation.6 | async-start | bytes 37748736 | tf_op jit(solution)/shard_map/all_gather | solution.py:80
  34.6 713.4 %all-gather.53.cloned.1.call-start = ((), (), s32[]{:S(2)}) async-start(), calls=%async_computation.8 | async-start | bytes 9437184 | tf_op jit(solution)/shard_map/all_gather | solution.py:80
  35.4 764.7 %all-gather.55.cloned.1.call-start = ((), (), s32[]{:S(2)}) async-start(), calls=%async_computation.9 | async-start | bytes 9437184 | tf_op jit(solution)/shard_map/all_gather | solution.py:80
  36.1 815.8 %all-gather.51.cloned.1.call-start = ((), (), s32[]{:S(2)}) async-start(), calls=%async_computation.7 | async-start | bytes 9437184 | tf_op jit(solution)/shard_map/all_gather | solution.py:80
  36.7 867.2 %all-gather.57.cloned.1.call-start = ((), (), s32[]{:S(2)}) async-start(), calls=%async_computation.10 | async-start | bytes 9437184 | tf_op jit(solution)/shard_map/all_gather | solution.py:80
  37.4 1025.3 %all-gather.59.cloned.1.call-start = ((), (), s32[]{:S(2)}) async-start(), calls=%async_computation.11 | async-start | bytes 37748736 | tf_op jit(solution)/shard_map/all_gather | solution.py:80
  38.0 1183.6 %all-gather.61.cloned.1.call-start = ((), (), s32[]{:S(2)}) async-start(), calls=%async_computation.12 | async-start | bytes 37748736 | tf_op jit(solution)/shard_map/all_gather | solution.py:80
  38.1 12.0 copy-start.26
  38.1 20.9 %copy-start.27 = (bf16[2,256]{1,0:T(2,128)(2,1)S(1)}, bf16[2,256]{1,0:T(2,128)(2,1)}, u32[]{:S(2)}) copy-start(bf16[2,256]{1,0:T(2,128)(2,1)} %param.22) | copy-start | bytes 3076
  38.1 28.8 %copy-start.28 = (bf16[2,256]{1,0:T(2,128)(2,1)S(1)}, bf16[2,256]{1,0:T(2,128)(2,1)}, u32[]{:S(2)}) copy-start(bf16[2,256]{1,0:T(2,128)(2,1)} %param.23) | copy-start | bytes 3076
  38.1 75.4 %copy-start.8 = (bf16[2,256,2048]{2,1,0:T(8,128)(2,1)S(1)}, bf16[2,256,2048]{2,1,0:T(8,128)(2,1)}, u32[]{:S(2)}) copy-start(bf16[2,256,2048]{2,1,0:T(8,128)(2,1)} %param.12) | copy-start | bytes 6291460
  38.8 1341.6 %all-gather.63.cloned.1.call-start = ((), (), s32[]{:S(2)}) async-start(), calls=%async_computation.13 | async-start | bytes 37748736 | tf_op jit(solution)/shard_map/all_gather | solution.py:80
  112.9 79.7 %copy-start.18 = (pred[256,256]{0,1:T(8,128)(4,1)}, pred[256,256]{0,1:T(8,128)(4,1)S(1)}, u32[]{:S(2)}) copy-start(pred[256,256]{0,1:T(8,128)(4,1)S(1)} %iota_compare_fusion) | copy-start | bytes 196612
  113.4 69.5 %copy-start.14 = (f32[256,64]{1,0:T(8,128)}, f32[256,64]{1,0:T(8,128)S(1)}, u32[]{:S(2)}) copy-start(f32[256,64]{1,0:T(8,128)S(1)} %get-tuple-element.47) | copy-start | bytes 196612
  113.4 69.5 %copy-start.16 = (f32[256,64]{1,0:T(8,128)}, f32[256,64]{1,0:T(8,128)S(1)}, u32[]{:S(2)}) copy-start(f32[256,64]{1,0:T(8,128)S(1)} %get-tuple-element.48) | copy-start | bytes 196612
  167.7 10.2 copy-start.3
  219.6 8.4 copy-start.9
  229.2 307.9 %copy-start.6 = (bf16[512,2048]{1,0:T(8,128)(2,1)}, bf16[512,2048]{1,0:T(8,128)(2,1)S(1)}, u32[]{:S(2)}) copy-start(bf16[512,2048]{1,0:T(8,128)(2,1)S(1)} %fusion.67) | copy-start | bytes 6291460
  562.7 157.9 %copy-start.24 = (f32[1,2048]{1,0:T(1,128)S(1)}, f32[1,2048]{1,0:T(1,128)}, u32[]{:S(2)}) copy-start(f32[1,2048]{1,0:T(1,128)} %convert_element_type.207) | copy-start | bytes 24580
  696.0 24.7 %copy-start.7 = (bf16[512,2048]{1,0:T(8,128)(2,1)S(1)}, bf16[512,2048]{1,0:T(8,128)(2,1)}, u32[]{:S(2)}) copy-start(bf16[512,2048]{1,0:T(8,128)(2,1)} %copy-done.6) | copy-start | bytes 6291460
  721.9 130.0 %copy-start.4 = (bf16[512,2048]{1,0:T(8,128)(2,1)}, bf16[512,2048]{1,0:T(8,128)(2,1)S(1)}, u32[]{:S(2)}) copy-start(bf16[512,2048]{1,0:T(8,128)(2,1)S(1)} %fusion.71) | copy-start | bytes 6291460
  721.9 34.4 %copy-start.23 = (f32[1,2048]{1,0:T(1,128)S(1)}, f32[1,2048]{1,0:T(1,128)}, u32[]{:S(2)}) copy-start(f32[1,2048]{1,0:T(1,128)} %convert_element_type.208) | copy-start | bytes 24580
  759.8 48.5 %copy-start.22 = (f32[1,2048]{1,0:T(1,128)S(1)}, f32[1,2048]{1,0:T(1,128)}, u32[]{:S(2)}) copy-start(f32[1,2048]{1,0:T(1,128)} %convert_element_type.209) | copy-start | bytes 24580
  903.9 8.6 copy-start.5
  903.9 8.6 copy-start.21
  1247.5 156.9 %copy-start.20 = (f32[1,2048]{1,0:T(1,128)S(1)}, f32[1,2048]{1,0:T(1,128)}, u32[]{:S(2)}) copy-start(f32[1,2048]{1,0:T(1,128)} %convert_element_type.211) | copy-start | bytes 24580
  (11 other events, 26.2 us)
Sparse Core Ops, SparseCore 0:
  10.0 53.1 all-gather.38
  65.1 50.5 all-gather.40
  117.5 50.1 all-gather.36
  169.4 50.1 all-gather.42
  221.3 157.0 all-gather.44
  380.0 157.0 all-gather.46
  538.9 157.0 all-gather.48
  697.8 50.1 all-gather.52
  749.9 50.1 all-gather.54
  801.7 50.1 all-gather.50
  853.8 50.1 all-gather.56
  905.6 157.0 all-gather.58
  1064.5 157.0 all-gather.60
  1223.3 157.0 all-gather.62
where the time goes:
time: 1420 us; the launch traced here: 1410 us
  waiting for transfers between devices  1010 us (71%)
  matrix products  228 us (16%)
  blocking collectives  70.4 us (5%)
  local copies, waits for them, and re-layouts  59.9 us (4%)
  other arithmetic  28.4 us (2%)
    all_gather x14, waiting for transfers between devices, gather_rows(): return lax.all_gather(arr_w[layer_idx], 'fsdp', axis=0, tiled=True)  1010 us
    dot_general x14, matrix products, dot_bf16(): jnp.dot(left, right, preferred_element_type=jnp.float32)  218 us
    all_gather x8, blocking collectives, gather_rows(): return lax.all_gather(arr_w[layer_idx], 'fsdp', axis=0, tiled=True)  70.4 us
  transfers between devices with their start and end apart: 14, of which 12 were waited for; matrix products, arithmetic and copies ran while one was open for 20% of the time, Pallas kernels for 0%

commit v1 on v0

v1 whole, which is shorter than its diff:
```python
import functools

import jax
import jax.numpy as jnp
import numpy as np
from jax import lax
from jax.experimental import pallas as pl
from jax.experimental.pallas import tpu as pltpu
from jax.sharding import PartitionSpec as P

HEAD_DIM = 128
EPS = 1e-6
THETA = 500000.0
SEQ = 256
D = 2048
ROWS = 512
N_BLK = 8
BLK = 256
PER_LAYER = 16
N_CHUNK = 32
PLANE = 176
ZP = 80
VIA_X = 80
VIA_Y = PLANE - VIA_X
A_OWN, A_FIRST, A_DIAG, A_PAIR = 6, 4, 3, 1
SLOTS = 4
TILE = 512
N_TILE = D // TILE
RB = 32

K_X, K_Y, K_P0, K_DX, K_DY, K_ZX, K_ZY, K_ZD, K_P1, K_P2, K_P3 = range(11)
N_KIND = 11
KIND_ROWS = (PLANE, PLANE, BLK, VIA_X, VIA_Y, ZP, ZP, ZP, BLK, BLK, BLK)


def rope_tables():
    pos = np.arange(SEQ, dtype=np.float64)
    inv = THETA ** (-2.0 * np.arange(HEAD_DIM // 2, dtype=np.float64) / HEAD_DIM)
    ang = pos[:, None] * inv[None, :]
    cos, sin = np.cos(ang), np.sin(ang)
    return (np.concatenate([cos, cos], 1).astype(np.float32), np.concatenate([-sin, sin], 1).astype(np.float32))


def kernel(x_hbm, cos_ref, sin_ref, gain_ref, wq, wk, wv, wo, wg, wu, wd, out_hbm, full, act, acc, wt, gains, send_sem, recv_sem, wt_sem, gs_sem, gr_sem, io_sem):
    zz = lax.axis_index('dp')
    me = lax.axis_index('fsdp')
    cc = me % 2
    xx = (me // 2) % 2
    yy = me // 4

    def at(y, x, c):
        return y * 4 + x * 2 + c

    f_p = at(yy, xx, 1 - cc)
    f_x = at(yy, 1 - xx, cc)
    f_y = at(1 - yy, xx, cc)
    f_d = at(1 - yy, 1 - xx, cc)
    dev_p, dev_x, dev_y, dev_z = (zz, f_p), (zz, f_x), (zz, f_y), (1 - zz, me)

    x_copy = pltpu.make_async_copy(x_hbm, act.at[0], io_sem)
    x_copy.start()

    barrier = pltpu.get_barrier_semaphore()
    for k in range(1, N_BLK):
        pl.semaphore_signal(barrier, inc=1, device_id=(zz, (me + k) % N_BLK), device_id_type=pl.DeviceIdType.MESH)
    pl.semaphore_signal(barrier, inc=1, device_id=dev_z, device_id_type=pl.DeviceIdType.MESH)
    pl.semaphore_wait(barrier, N_BLK)

    gain_copies = []
    for k in range(1, N_BLK):
        cp = pltpu.make_async_remote_copy(gain_ref, gains.at[me], gs_sem.at[k], gr_sem.at[k], device_id=(zz, (me + k) % N_BLK), device_id_type=pl.DeviceIdType.MESH)
        cp.start()
        gain_copies.append(cp)

    def m16(v):
        return pl.multiple_of(v, 16)

    off_plane = m16(ZP * zz)
    off_dx = m16(ZP * zz)
    off_dy = m16(ZP * zz + VIA_X)
    off_z = m16(PLANE * zz)

    def own(i, fn):
        la = i // PER_LAYER
        t = i % PER_LAYER
        g = (t - 4) // 2
        for k, w in enumerate((wq, wk, wv, wo)):
            pl.when(t == k)(functools.partial(fn, w.at[la]))
        mid = (t >= 4) & (t < 12)
        cols = pl.ds(pl.multiple_of(g * D, D), D)

        @pl.when(mid & (t % 2 == 0))
        def _():
            fn(wg.at[la, :, cols])

        @pl.when(mid & (t % 2 == 1))
        def _():
            fn(wu.at[la, :, cols])

        @pl.when(t >= 12)
        def _():
            fn(wd.at[la, pl.ds(pl.multiple_of((t - 12) * BLK, BLK), BLK), :])

    def remote(kind, i, src, dst, dev):
        return pltpu.make_async_remote_copy(src, dst, send_sem.at[kind, i % SLOTS], recv_sem.at[kind, i], device_id=dev, device_id_type=pl.DeviceIdType.MESH)

    def drain(kind, i):
        piece = full.at[0, 0, pl.ds(0, KIND_ROWS[kind]), :]
        remote(kind, i, piece, piece, dev_p).wait_send()

    def arrived(kind, i):
        piece = full.at[0, 0, pl.ds(0, KIND_ROWS[kind]), :]
        remote(kind, i, piece, piece, dev_p).wait_recv()

    def push(kind, i, blk, off, dev):
        pl.when(i >= SLOTS)(functools.partial(drain, kind, i - SLOTS))
        piece = full.at[i, blk, pl.ds(off, KIND_ROWS[kind]), :]
        remote(kind, i, piece, piece, dev).start()

    def stage_own(i):
        for kind in (K_X, K_Y, K_P0):
            pl.when(i >= SLOTS)(functools.partial(drain, kind, i - SLOTS))

        def go(src):
            part = pl.ds(off_plane, PLANE)
            remote(K_X, i, src.at[part, :], full.at[i, me, part, :], dev_x).start()
            remote(K_Y, i, src.at[part, :], full.at[i, me, part, :], dev_y).start()
            remote(K_P0, i, src, full.at[i, me], dev_p).start()

        own(i, go)

    def stage_first(i):
        arrived(K_X, i)
        push(K_ZX, i, f_x, off_z, dev_z)
        push(K_DY, i, f_x, off_dy, dev_y)
        arrived(K_Y, i)
        push(K_ZY, i, f_y, off_z, dev_z)
        push(K_DX, i, f_y, off_dx, dev_x)

    def stage_diag(i):
        arrived(K_DX, i)
        arrived(K_DY, i)
        push(K_ZD, i, f_d, off_z, dev_z)

    def stage_pair(i):
        arrived(K_ZX, i)
        push(K_P1, i, f_x, 0, dev_p)
        arrived(K_ZY, i)
        push(K_P2, i, f_y, 0, dev_p)
        arrived(K_ZD, i)
        push(K_P3, i, f_d, 0, dev_p)

    def load_tile(i, n):
        slot = n % 2
        cols = pl.ds(n * TILE, TILE)

        def own_block(src):
            pltpu.make_async_copy(src.at[:, cols], wt.at[slot, me], wt_sem.at[slot]).start()

        own(i, own_block)
        for k in range(1, N_BLK):
            b = (me + k) % N_BLK
            pltpu.make_async_copy(full.at[i, b, :, cols], wt.at[slot, b], wt_sem.at[slot]).start()

    def wait_tile(n):
        slot = n % 2
        pltpu.make_async_copy(full.at[0, :, :, pl.ds(0, TILE)], wt.at[slot], wt_sem.at[slot]).wait()

    def gain_row(la, k):
        return jnp.concatenate([gains[f, pl.ds(la * 4 + k, 1), :] for f in range(N_BLK)], axis=1)

    def normed(r0, gain):
        a = acc[pl.ds(r0, RB), :].astype(jnp.bfloat16).astype(jnp.float32)
        ms = jnp.mean(a * a, axis=-1, keepdims=True)
        return a * lax.rsqrt(ms + EPS) * gain

    def rows(body):
        def step(r, carry):
            body(pl.multiple_of(r * RB, RB))
            return carry

        lax.fori_loop(0, ROWS // RB, step, 0)

    def norm_rope(la, k, dst):
        gain = gain_row(la, k)

        def body(r0):
            v = normed(r0, gain)
            p0 = pl.multiple_of(r0 % SEQ, RB)
            c = cos_ref[pl.ds(p0, RB), :]
            s = sin_ref[pl.ds(p0, RB), :]
            for h in range(D // HEAD_DIM):
                part = v[:, h * HEAD_DIM:(h + 1) * HEAD_DIM]
                turned = pltpu.roll(part, HEAD_DIM // 2, 1)
                act[dst, pl.ds(r0, RB), h * HEAD_DIM:(h + 1) * HEAD_DIM] = (part * c + turned * s).astype(jnp.bfloat16)

        rows(body)

    def attention():
        row = lax.broadcasted_iota(jnp.int32, (SEQ, SEQ), 0)
        col = lax.broadcasted_iota(jnp.int32, (SEQ, SEQ), 1)
        causal = row >= col

        def step(h, carry):
            lanes = pl.ds(pl.multiple_of(h * HEAD_DIM, HEAD_DIM), HEAD_DIM)
            for b in range(ROWS // SEQ):
                sq = pl.ds(b * SEQ, SEQ)
                q, k, v = act[1, sq, lanes], act[2, sq, lanes], act[3, sq, lanes]
                s = lax.dot_general(q, k, (((1,), (1,)), ((), ())), preferred_element_type=jnp.float32) * (HEAD_DIM ** -0.5)
                s = jnp.where(causal, s, -jnp.inf)
                e = jnp.exp(s - jnp.max(s, axis=-1, keepdims=True))
                p = (e / jnp.sum(e, axis=-1, keepdims=True)).astype(jnp.bfloat16)
                act[1, sq, lanes] = jnp.dot(p, v, preferred_element_type=jnp.float32).astype(jnp.bfloat16)
            return carry

        lax.fori_loop(0, D // HEAD_DIM, step, 0)

    def residual(la, k, src, dst):
        gain = gain_row(la, k)

        def body(r0):
            rr = pl.ds(r0, RB)
            act[dst, rr, :] = (act[src, rr, :].astype(jnp.float32) + normed(r0, gain)).astype(jnp.bfloat16)

        rows(body)

    def compute(i):
        la = i // PER_LAYER
        t = i % PER_LAYER
        lhs = jnp.where(t < 3, 0, jnp.where(t == 3, 1, jnp.where(t < 12, 4, t - 7)))
        keep = t > 12
        load_tile(i, 0)
        for n in range(N_TILE):
            if n + 1 < N_TILE:
                load_tile(i, n + 1)
            wait_tile(n)
            cols = slice(n * TILE, (n + 1) * TILE)
            prod = jnp.dot(act[lhs], wt[n % 2].reshape(D, TILE), preferred_element_type=jnp.float32)
            acc[:, cols] = jnp.where(keep, acc[:, cols], 0.0) + prod

        @pl.when(i == 0)
        def _():
            for cp in gain_copies:
                cp.wait()
            gains[pl.ds(me, 1)] = gain_ref[...][None]

        @pl.when(t == 0)
        def _():
            norm_rope(la, 0, 1)

        @pl.when(t == 1)
        def _():
            norm_rope(la, 1, 2)

        @pl.when(t == 2)
        def _():
            def body(r0):
                act[3, pl.ds(r0, RB), :] = acc[pl.ds(r0, RB), :].astype(jnp.bfloat16)

            rows(body)
            attention()

        @pl.when(t == 3)
        def _():
            residual(la, 2, 0, 4)

        mid = (t >= 4) & (t < 12)

        @pl.when(mid & (t % 2 == 0))
        def _():
            def body(r0):
                act[2, pl.ds(r0, RB), :] = acc[pl.ds(r0, RB), :].astype(jnp.bfloat16)

            rows(body)

        @pl.when(mid & (t % 2 == 1))
        def _():
            g = (t - 4) // 2

            def body(r0):
                rr = pl.ds(r0, RB)
                for c in range(N_BLK):
                    cols = slice(c * BLK, (c + 1) * BLK)
                    gate = act[2, rr, cols].astype(jnp.float32)
                    up = acc[rr, cols].astype(jnp.bfloat16).astype(jnp.float32)
                    val = (jax.nn.silu(gate) * up).astype(jnp.bfloat16)
                    lanes = pl.ds(pl.multiple_of((2 * g + c // 4) * BLK, BLK), BLK)
                    act[5 + c % 4, rr, lanes] = val

            rows(body)

        @pl.when(t == 15)
        def _():
            residual(la, 3, 4, 0)

    x_copy.wait()

    def step(it, carry):
        i = it - A_OWN
        for ahead, stage in ((A_OWN, stage_own), (A_FIRST, stage_first), (A_DIAG, stage_diag), (A_PAIR, stage_pair)):
            j = i + ahead
            pl.when((j >= 0) & (j < N_CHUNK))(functools.partial(stage, j))

        @pl.when(i >= 0)
        def _():
            for kind in (K_P0, K_P1, K_P2, K_P3):
                arrived(kind, i)
            compute(i)

        return carry

    lax.fori_loop(0, N_CHUNK + A_OWN, step, 0)

    for kind in range(N_KIND):
        for i in range(N_CHUNK - SLOTS, N_CHUNK):
            drain(kind, i)
    out_copy = pltpu.make_async_copy(act.at[0], out_hbm, io_sem)
    out_copy.start()
    out_copy.wait()


def solution(mesh):
    cos_np, sin_np = rope_tables()
    hbm = pl.BlockSpec(memory_space=pl.ANY)
    vmem = pl.BlockSpec(memory_space=pltpu.VMEM)

    def local_fn(tokens, weights, gain_vecs):
        gains = jnp.stack(gain_vecs, axis=1).reshape(8, BLK).astype(jnp.float32)
        flat = tokens.reshape(ROWS, D)
        out, _ = pl.pallas_call(
            kernel,
            out_shape=(jax.ShapeDtypeStruct((ROWS, D), jnp.bfloat16), jax.ShapeDtypeStruct((N_CHUNK, N_BLK, BLK, D), jnp.bfloat16)),
            in_specs=[hbm, vmem, vmem, vmem] + [hbm] * 7,
            out_specs=(hbm, hbm),
            scratch_shapes=[
                pltpu.VMEM((9, ROWS, D), jnp.bfloat16),
                pltpu.VMEM((ROWS, D), jnp.float32),
                pltpu.VMEM((2, N_BLK, BLK, TILE), jnp.bfloat16),
                pltpu.VMEM((N_BLK, 8, BLK), jnp.float32),
                pltpu.SemaphoreType.DMA((N_KIND, SLOTS)),
                pltpu.SemaphoreType.DMA((N_KIND, N_CHUNK)),
                pltpu.SemaphoreType.DMA((2,)),
                pltpu.SemaphoreType.DMA((N_BLK,)),
                pltpu.SemaphoreType.DMA((N_BLK,)),
                pltpu.SemaphoreType.DMA,
            ],
            compiler_params=pltpu.CompilerParams(collective_id=0, has_side_effects=True, vmem_limit_bytes=60 * 1024 * 1024),
        )(flat, jnp.asarray(cos_np), jnp.asarray(sin_np), gains, *weights)
        return out.reshape(tokens.shape)

    mapped = jax.shard_map(local_fn, mesh=mesh, in_specs=(P(('dp', 'fsdp')), P(None, 'fsdp'), P(None, 'fsdp')), out_specs=P(('dp', 'fsdp')), check_vma=False)

    def run(tokens, w_query, w_key, w_value, w_out, w_gate, w_up, w_down, g_query, g_key, g_attn, g_mlp):
        return mapped(tokens, (w_query, w_key, w_value, w_out, w_gate, w_up, w_down), (g_query, g_key, g_attn, g_mlp))

    return run
```

time: 1420 us -> 822 us (0.58)
  waiting for transfers between devices: 1010 us -> 0 us
  Pallas kernels: 0 us -> 814 us
  matrix products: 228 us -> 0 us
  blocking collectives: 70.4 us -> 0 us
  local copies, waits for them, and re-layouts: 59.9 us -> 6.5 us
  other arithmetic: 28.4 us -> 0.02 us
    all_gather x14 -> x0, waiting for transfers between devices: 1010 us -> none  [gather_rows(): return lax.all_gather(arr_w[layer_idx], 'fsdp', axis=0, tiled=True)]
    pallas_call x0 -> x1, Pallas kernels: none -> 814 us  [local_fn(): pl.pallas_call(kernel, out_shape=(jax.ShapeDtypeStruct((ROWS, D), jnp.bfl...]
    dot_general x18 -> x0, matrix products: 228 us -> none  [the longest x14 218 us: dot_bf16(): jnp.dot(left, right, preferred_element_type=jnp.float32)]
    all_gather x8 -> x0, blocking collectives: 70.4 us -> none  [gather_rows(): return lax.all_gather(arr_w[layer_idx], 'fsdp', axis=0, tiled=True)]
    slice x14 -> x0, local copies, waits for them, and re-layouts: 34.4 us -> none  [the longest x11 27.6 us: gather_rows(): return lax.all_gather(arr_w[layer_idx], 'fsdp', axis=0, tiled=True)]
    unnamed x64 -> x1, local copies, waits for them, and re-layouts: 18.6 us -> 3.16 us
  transfers between devices with their start and end apart: 14 -> 0, of which waited for: 12 -> 0; matrix products, arithmetic and copies ran while one was open for 20% -> 0% of each run, Pallas kernels for 0% -> 0%
where the time goes in v1:
time: 822 us; the launch traced here: 821 us
  Pallas kernels  814 us (99%)
    pallas_call x1, Pallas kernels, local_fn(): pl.pallas_call(kernel, out_shape=(jax.ShapeDtypeStruct((ROWS, D), jnp.bfl...  814 us

profile of v1, /device:TPU:0, one launch (start us, length us, event | category | flops | bytes accessed | tf_op | source)
XLA Modules:
  0.0 820.6 jit_solution(1949001337787681812)
XLA Ops:
  0.0 0.7 copy.16
  0.7 0.7 copy.17
  1.4 0.7 copy.18
  2.0 0.7 copy.19
  2.7 0.6 reshape.11.gain_ref
  3.4 814.1 %shard_map.136 = (bf16[512,2048]{1,0:T(8,128)(2,1)}, bf16[32,8,256,2048]{3,2,1,0:T(8,128)(2,1)}) custom-call(bf16[512,2048]{1,0:T(8,128)(2,1)} %bitcast.6, f32[256,128]{1,0:T(8,128)} %constant.4.clone.cos_ref, f32[256,128]{1,0:T(8,128)} %constant.5.clone.sin_ref, f32[8,256]{1,0:T(8,128)} %reshape.11.gain_ref, bf16[2,256,2048]{2,1,0:T(8,128)(2,1)} %wq.1, ...), custom_call_target="tpu_custom_call" | custom-call | tf_op jit(solution)/shard_map/pallas_call | solution.py:330
  817.4 3.2 copy.21
  (1 shorter events, 0.0 us)

commit v2 on v0

v2 whole, which is shorter than its diff:
```python
import functools

import jax
import jax.numpy as jnp
import numpy as np
from jax import lax
from jax.experimental import pallas as pl
from jax.experimental.pallas import tpu as pltpu
from jax.sharding import PartitionSpec as P

HEAD_DIM = 128
EPS = 1e-6
THETA = 500000.0
SEQ = 256
D = 2048
ROWS = 512
N_BLK = 8
BLK = 256
TILE = 512
N_TILE = D // TILE
RB = 32
MESH = pl.DeviceIdType.MESH

UNIT = 22.5 / 256
LAT = 2.5
PAIR = 4.0
FLOW = {'A': (160, 128, 80, 48, 0), 'B': (128, 192, 0, 128, 0), 'H': (256, 128, 0, 128, 160), 'G': (224, 176, 0, 128, 192)}
ITEMS = ['A'] * 4 + ['H'] * 4 + ['B'] * 4 + ['G'] * 3 + ['B'] * 3
N_H = (4, 3)
BACKLOG = 18.0
COST = {'mm': 5.0, 'at': 7.0, 'h': 12.0, 'wgu': 9.0, 'wd': 9.0, 'fin': 3.0}


def slots(nh=(4, 3)):
    out = []
    for k in range(3):
        out.append(('mm', k, 0, k, 2))
    base = 4
    attn = (0, 4 + nh[0])
    for la in range(2):
        for s in range(2):
            if la:
                for k in range(3):
                    out.append(('mm', attn[1] + k, 1, k, s))
            for q in range(2):
                out.append(('at', 0, la, q, s))
            out.append(('mm', attn[la] + 3, la, 3, s))
        h0 = attn[la] + 4
        if la == 0:
            for j in range(nh[0]):
                for s in range(2):
                    out.append(('h', h0 + j, 0, j, s))
        else:
            for s in range(2):
                for j in range(nh[1]):
                    out.append(('h', h0 + j, 1, j, s))
            w0 = h0 + nh[1]
            if nh[1] < 4:
                out.append(('wgu', w0, 1, 0, 2))
                out.append(('wgu', w0 + 1, 1, 1, 2))
                out.append(('wd', w0 + 2, 1, 4, 2))
        for s in range(2):
            out.append(('fin', 0, la, 0, s))
    return out


def schedule(thr=20.0, nh=(4, 3)):
    sl = slots(nh)
    t = 0.0
    free = dict(x=0.0, y=0.0, z=0.0, p=0.0)
    arr = {}
    prog = []
    busy = dict(x=0.0, y=0.0, z=0.0, p=0.0)

    def send(link, dur, key):
        s = max(free[link], t)
        free[link] = s + dur
        busy[link] += dur
        arr[key] = free[link] + LAT

    xq = [i for i in range(len(ITEMS))]
    yq = []
    for i, f in enumerate(ITEMS):
        yq.append(('oy', i))
        if f in 'HG':
            yq.append(('on', i))
    pend = []
    for i, f in enumerate(ITEMS):
        px, py, dx, dy, pn = FLOW[f]
        pend.append((('fx', i), [('X', i)]))
        pend.append((('fy', i), [('Y', i)]))
        pend.append((('fd', i), ([('DX', i)] if dx else []) + [('DY', i)]))
        if px < 256:
            pend.append((('px', i), [('X', i), ('ZX', i)]))
        pend.append((('py', i), [('Y', i), ('ZY', i)]))
        pend.append((('pd', i), ([('DX', i)] if dx else []) + [('DY', i), ('ZD', i)]))
        if pn:
            pend.append((('fn', i), [('N', i)]))
            pend.append((('pn', i), [('N', i), ('ZN', i)]))

    def run(op):
        if op[0] in ('ag', 'rs'):
            units, key = (1, 'H') if op[0] == 'ag' else (2, 'R')
            send('x', units * 22.5, (key,) + op[1:])
            prog.append(op)
            return
        kind, i = op
        px, py, dx, dy, pn = FLOW[ITEMS[i]]
        if kind == 'ox':
            send('x', px * UNIT, ('X', i))
        elif kind == 'oy':
            send('y', py * UNIT, ('Y', i))
            send('p', PAIR, ('P0', i))
        elif kind == 'on':
            send('y', pn * UNIT, ('N', i))
            send('p', PAIR, ('Q0', i))
        elif kind == 'fx':
            if px < 256:
                send('z', (256 - px) * UNIT, ('ZX', i))
            else:
                send('p', PAIR, ('P1', i))
            send('y', dy * UNIT, ('DY', i))
        elif kind == 'fy':
            send('z', (256 - py) * UNIT, ('ZY', i))
            if dx:
                send('x', dx * UNIT, ('DX', i))
        elif kind == 'fd':
            send('z', (256 - dx - dy) * UNIT, ('ZD', i))
        elif kind == 'fn':
            send('z', (256 - pn) * UNIT, ('ZN', i))
        elif kind in ('px', 'py', 'pd'):
            send('p', PAIR, (dict(px='P1', py='P2', pd='P3')[kind], i))
        elif kind == 'pn':
            send('p', PAIR, ('Q1', i))
        prog.append(op)

    def needs(s):
        ty, it, la, ex, hf = s
        n = []
        if ty in ('mm', 'h', 'wgu', 'wd'):
            n += [('P%d' % k, it) for k in range(4)]
        if ty == 'h':
            n += [('Q%d' % k, it) for k in range(2)]
            n.append(('H', la, hf))
        if ty == 'fin':
            n.append(('R', la, hf))
        return n

    def after(s):
        ty, it, la, ex, hf = s
        if ty == 'mm' and ex < 3:
            return [('fin', la - 1, 0, hf)] if la else []
        if ty == 'at':
            return [('mm', la, k, hf if la else 2) for k in range(3)]
        if ty == 'mm':
            return [('at', la, q, hf) for q in range(2)]
        if ty == 'h':
            return [('mm', la, 3, hf)] + ([('h', la, ex - 1, hf)] if ex else [])
        if ty == 'wgu':
            return [('mm', la, 3, 0), ('mm', la, 3, 1)]
        if ty == 'wd':
            return [('wgu', la, 0, 2), ('wgu', la, 1, 2)] + [('h', la, nh[1] - 1, q) for q in range(2)]
        return [('h', la, nh[la] - 1, hf)] + ([('wd', la, 4, 2)] if la and nh[1] < 4 else [])

    done = set()
    todo = list(range(len(sl)))
    while todo:
        again = True
        while again:
            again = False
            for op, ns in list(pend):
                if all(arr.get(x, 1e9) <= t for x in ns):
                    pend.remove((op, ns))
                    run(op)
                    again = True
            if xq and free['x'] - t < thr:
                run(('ox', xq.pop(0)))
                again = True
            if yq and free['y'] - t < thr:
                run(yq.pop(0))
                again = True
        pick = None
        ev = [arr[x] for op, n2 in pend for x in n2 if x in arr]
        for k in todo:
            s = sl[k]
            if not all(x in done for x in after(s)):
                continue
            ns = needs(s)
            if all(arr.get(x, 1e9) <= t for x in ns):
                pick = k
                break
            ev += [arr[x] for x in ns if x in arr]
        if pick is not None:
            s = sl[pick]
            todo.remove(pick)
            prog.append(('slot', pick))
            t += COST[s[0]] * (2 if s[0] == 'mm' and s[4] == 2 else 1)
            done.add((s[0], s[2], s[3], s[4]))
            if s[0] == 'mm' and s[3] == 3:
                run(('ag', s[2], s[4]))
            if s[0] == 'h' and s[3] == nh[s[2]] - 1:
                run(('rs', s[2], s[4]))
            continue
        if xq:
            ev.append(free['x'] - thr + 0.01)
        if yq:
            ev.append(free['y'] - thr + 0.01)
        t = min(e for e in ev if e > t)
    assert not pend and not xq and not yq
    return sl, prog, t


def plan():
    sl, prog, _ = schedule(BACKLOG, N_H)
    order, lists, cur, seen = [], [], [], set()
    for op in prog:
        if op[0] != 'slot':
            cur.append(op)
            continue
        s = sl[op[1]]
        ty, it, la, ex, hf = s
        need = []
        if ty in ('mm', 'h', 'wgu', 'wd'):
            need += [('P%d' % k, it) for k in range(4)]
        if ty == 'h':
            need += [('Q%d' % k, it) for k in range(2)] + [('H', la, hf)]
            if la == 1 and ex == 0:
                cur.append(('drain', ('R', 0, hf)))
        if ty == 'fin':
            need.append(('R', la, hf))
        for key in need:
            if key not in seen:
                seen.add(key)
                cur.append(('wait', key))
        order.append(s)
        lists.append(cur)
        cur = []
    assert not cur or all(op[0] in ('ag', 'rs') for op in cur)
    return order, lists


def copy_keys():
    keys = []
    for i, f in enumerate(ITEMS):
        px, py, dx, dy, pn = FLOW[f]
        rows = {'X': px, 'Y': py, 'P0': BLK, 'DX': dx, 'DY': dy, 'ZX': BLK - px, 'ZY': BLK - py, 'ZD': BLK - dx - dy, 'P1': BLK, 'P2': BLK, 'P3': BLK}
        if pn:
            rows.update({'N': pn, 'ZN': BLK - pn, 'Q0': BLK, 'Q1': BLK})
        keys += [((k, i), r) for k, r in rows.items() if r]
    for la in range(2):
        for s in range(2):
            keys += [(('H', la, s), BLK), (('R', la, s), 0)]
    return keys


KEYS = copy_keys()
SID = {k: n for n, (k, _) in enumerate(KEYS)}
KROWS = dict(KEYS)
H_ITEMS = [i for i, f in enumerate(ITEMS) if FLOW[f][4]]
ATTN0 = (0, 4 + N_H[0])
W_ITEM = 8 + N_H[0] + N_H[1]


def rope_tables():
    pos = np.arange(SEQ, dtype=np.float64)
    inv = THETA ** (-2.0 * np.arange(HEAD_DIM // 2, dtype=np.float64) / HEAD_DIM)
    ang = pos[:, None] * inv[None, :]
    cos, sin = np.cos(ang), np.sin(ang)
    return (np.concatenate([cos, cos], 1).astype(np.float32), np.concatenate([-sin, sin], 1).astype(np.float32))


def kernel(x_hbm, cos_ref, sin_ref, gain_ref, wq, wk, wv, wo, wg, wu, wd, out_hbm, full, full_n, act, h2, mj, acc, rs, wt, gains, send_sem, recv_sem, wt_sem, gs_sem, gr_sem, io_sem):
    zz = lax.axis_index('dp')
    me = lax.axis_index('fsdp')
    cc = me % 2
    xx = (me // 2) % 2
    yy = me // 4

    def at(y, x, c):
        return y * 4 + x * 2 + c

    f_p = at(yy, xx, 1 - cc)
    f_x = at(yy, 1 - xx, cc)
    f_y = at(1 - yy, xx, cc)
    f_d = at(1 - yy, 1 - xx, cc)
    n_me, n_y = yy * 2 + cc, (1 - yy) * 2 + cc
    dev_p, dev_x, dev_y, dev_z = (zz, f_p), (zz, f_x), (zz, f_y), (1 - zz, me)

    x_copy = pltpu.make_async_copy(x_hbm, act.at[0], io_sem)
    x_copy.start()

    barrier = pltpu.get_barrier_semaphore()
    for k in range(1, N_BLK):
        pl.semaphore_signal(barrier, inc=1, device_id=(zz, (me + k) % N_BLK), device_id_type=MESH)
    pl.semaphore_signal(barrier, inc=1, device_id=dev_z, device_id_type=MESH)
    pl.semaphore_wait(barrier, N_BLK)

    def m16(v):
        return pl.multiple_of(v, 16)

    def m256(v):
        return pl.multiple_of(v, 256)

    def remote(key, src, dst, dev):
        return pltpu.make_async_remote_copy(src, dst, send_sem.at[SID[key]], recv_sem.at[SID[key]], device_id=dev, device_id_type=MESH)

    def same_size(key):
        piece = rs.at[0, 0] if key[0] == 'R' else full.at[0, 0, pl.ds(0, KROWS[key]), :]
        return remote(key, piece, piece, dev_p)

    def arrived(key):
        same_size(key).wait_recv()

    def own_pieces(i, side):
        la = int(i >= ATTN0[1])
        if i >= W_ITEM:
            if i == W_ITEM + 2:
                return [(wd.at[la, pl.ds(3 * BLK, BLK), :], 0, D)]
            cols = [1024 * (4 * (i - W_ITEM) + n) + 3 * BLK for n in range(4)]
        elif i in H_ITEMS:
            j = i - ATTN0[la] - 4
            cols = [m256(4096 * (n // 2) + 2048 * side + 1024 * (n % 2) + BLK * j) for n in range(4)]
        else:
            return [((wq, wk, wv, wo)[i - ATTN0[la]].at[la], 0, D)]
        out = []
        for n, c in enumerate(cols):
            out.append((wg.at[la, :, pl.ds(c, BLK)], n * TILE, BLK))
            out.append((wu.at[la, :, pl.ds(c, BLK)], n * TILE + BLK, BLK))
        return out

    def send_own(key, i, side, off, rows, dev):
        part = pl.ds(off, rows)
        for src, c0, nc in own_pieces(i, side):
            remote(key, src.at[part, :], full.at[i, me, part, pl.ds(c0, nc)], dev).start()

    def push(key, i, blk, off, dev):
        piece = full.at[i, blk, pl.ds(off, KROWS[key]), :]
        remote(key, piece, piece, dev).start()

    def push_n(key, i, off, dev):
        piece = full_n.at[H_ITEMS.index(i), n_y, pl.ds(off, KROWS[key]), :]
        remote(key, piece, piece, dev).start()

    def transfer(op):
        kind = op[0]
        if kind == 'wait':
            arrived(op[1])
        elif kind == 'drain':
            same_size(op[1]).wait_send()
        elif kind == 'ag':
            la, s = op[1:]
            remote(('H', la, s), h2.at[la, s, pl.ds(0, SEQ), :], h2.at[la, s, pl.ds(SEQ, SEQ), :], dev_x).start()
        elif kind == 'rs':
            la, s = op[1:]
            remote(('R', la, s), acc.at[s, pl.ds(SEQ, SEQ), :], rs.at[la, s], dev_x).start()
        else:
            i = op[1]
            px, py, dx, dy, pn = FLOW[ITEMS[i]]
            off_d = m16((BLK - dx - dy) * zz)
            if kind == 'ox':
                send_own(('X', i), i, 1 - xx, m16((BLK - px) * zz), px, dev_x)
            elif kind == 'oy':
                send_own(('Y', i), i, xx, m16((BLK - py) * zz), py, dev_y)
                send_own(('P0', i), i, xx, 0, BLK, dev_p)
            elif kind == 'fx':
                arrived(('X', i))
                if px < BLK:
                    push(('ZX', i), i, f_x, m16(px * zz), dev_z)
                else:
                    push(('P1', i), i, f_x, 0, dev_p)
                push(('DY', i), i, f_x, m16(off_d + dx), dev_y)
            elif kind == 'fy':
                arrived(('Y', i))
                push(('ZY', i), i, f_y, m16(py * zz), dev_z)
                if dx:
                    push(('DX', i), i, f_y, off_d, dev_x)
            elif kind == 'fd':
                if dx:
                    arrived(('DX', i))
                arrived(('DY', i))
                push(('ZD', i), i, f_d, m16((dx + dy) * zz), dev_z)
            elif kind == 'px':
                arrived(('ZX', i))
                push(('P1', i), i, f_x, 0, dev_p)
            elif kind == 'py':
                arrived(('ZY', i))
                push(('P2', i), i, f_y, 0, dev_p)
            elif kind == 'pd':
                arrived(('ZD', i))
                push(('P3', i), i, f_d, 0, dev_p)
            else:
                hn = H_ITEMS.index(i)
                la = int(i >= ATTN0[1])
                r0 = BLK * (i - ATTN0[la] - 4)
                if kind == 'on':
                    off = m16((BLK - pn) * zz)
                    remote(('N', i), wd.at[la, pl.ds(m16(r0 + off), pn), :], full_n.at[hn, n_me, pl.ds(off, pn), :], dev_y).start()
                    remote(('Q0', i), wd.at[la, pl.ds(r0, BLK), :], full_n.at[hn, n_me], dev_p).start()
                elif kind == 'fn':
                    arrived(('N', i))
                    push_n(('ZN', i), i, m16(pn * zz), dev_z)
                elif kind == 'pn':
                    arrived(('ZN', i))
                    push_n(('Q1', i), i, 0, dev_p)

    order, lists = plan()
    n_slot = len(order)

    def load(parts, slot):
        for src, dst in parts:
            pltpu.make_async_copy(src, dst, wt_sem.at[slot]).start()

    def others(i, n):
        slot = n % 2
        cols = pl.ds(n * TILE, TILE)
        load([(full.at[i, (me + k) % N_BLK, :, cols], wt.at[slot, (me + k) % N_BLK]) for k in range(1, N_BLK)], slot)

    def wait_tile(n, blocks=N_BLK):
        slot = n % 2
        part = wt.at[slot, pl.ds(0, blocks)]
        pltpu.make_async_copy(full.at[0, pl.ds(0, blocks), :, pl.ds(0, TILE)], part, wt_sem.at[slot]).wait()

    def load_mm(i, la, role, n):
        slot = n % 2
        cols = pl.ds(n * TILE, TILE)
        for k, w in enumerate((wq, wk, wv, wo)):
            pl.when(role == k)(functools.partial(load, [(w.at[la, :, cols], wt.at[slot, me])], slot))
        pl.when(role == 4)(functools.partial(load, [(wd.at[1, pl.ds(3 * BLK, BLK), cols], wt.at[slot, me])], slot))
        others(i, n)

    def load_gu(i, la, col, n):
        slot = n % 2
        c = pl.ds(m256(col(n)), BLK)
        load([(wg.at[la, :, c], wt.at[slot, me, :, pl.ds(0, BLK)]), (wu.at[la, :, c], wt.at[slot, me, :, pl.ds(BLK, BLK)])], slot)
        others(i, n)

    def load_dn(hn, la, j, n):
        slot = n % 2
        cols = pl.ds(n * TILE, TILE)
        parts = [(wd.at[la, pl.ds(m256(j * BLK), BLK), cols], wt.at[slot, n_me])]
        parts += [(full_n.at[hn, (n_me + k) % 4, :, cols], wt.at[slot, (n_me + k) % 4]) for k in range(1, 4)]
        load(parts, slot)

    def gain_row(la, k):
        return jnp.concatenate([gains[f, pl.ds(la * 4 + k, 1), :] for f in range(N_BLK)], axis=1)

    def scaled(v, gain):
        a = v.astype(jnp.bfloat16).astype(jnp.float32)
        ms = jnp.mean(a * a, axis=-1, keepdims=True)
        return a * lax.rsqrt(ms + EPS) * gain

    def rows(body):
        def step(r, carry):
            body(pl.multiple_of(r * RB, RB))
            return carry

        lax.fori_loop(0, SEQ // RB, step, 0)

    def act_rows(s, r0):
        return pl.ds(pl.multiple_of(s * SEQ + r0, RB), RB)

    def norm_rope(la, k, dst, s):
        gain = gain_row(la, k)

        def body(r0):
            v = scaled(acc[s, pl.ds(r0, RB), :], gain)
            c = cos_ref[pl.ds(r0, RB), :]
            sn = sin_ref[pl.ds(r0, RB), :]
            for h in range(D // HEAD_DIM):
                part = v[:, h * HEAD_DIM:(h + 1) * HEAD_DIM]
                turned = pltpu.roll(part, HEAD_DIM // 2, 1)
                act[dst, act_rows(s, r0), h * HEAD_DIM:(h + 1) * HEAD_DIM] = (part * c + turned * sn).astype(jnp.bfloat16)

        rows(body)

    def attention(q8, s):
        row = lax.broadcasted_iota(jnp.int32, (SEQ, SEQ), 0)
        col = lax.broadcasted_iota(jnp.int32, (SEQ, SEQ), 1)
        causal = row >= col
        sq = pl.ds(pl.multiple_of(s * SEQ, SEQ), SEQ)

        def step(h, carry):
            for u in range(2):
                lanes = pl.ds(pl.multiple_of((q8 * 8 + h * 2 + u) * HEAD_DIM, HEAD_DIM), HEAD_DIM)
                q, k, v = act[1, sq, lanes], act[2, sq, lanes], act[3, sq, lanes]
                sc = lax.dot_general(q, k, (((1,), (1,)), ((), ())), preferred_element_type=jnp.float32) * (HEAD_DIM ** -0.5)
                sc = jnp.where(causal, sc, -jnp.inf)
                e = jnp.exp(sc - jnp.max(sc, axis=-1, keepdims=True))
                p = (e / jnp.sum(e, axis=-1, keepdims=True)).astype(jnp.bfloat16)
                act[1, sq, lanes] = jnp.dot(p, v, preferred_element_type=jnp.float32).astype(jnp.bfloat16)
            return carry

        lax.fori_loop(0, 4, step, 0)

    def mm(i, la, role, hf):
        s0 = jnp.where(hf == 2, 0, hf)
        s1 = jnp.where(hf == 2, 2, hf + 1)
        lhs = jnp.where(role < 3, 0, jnp.where(role == 3, 1, 4))
        load_mm(i, la, role, 0)
        for n in range(N_TILE):
            if n + 1 < N_TILE:
                load_mm(i, la, role, n + 1)
            wait_tile(n)
            cols = slice(n * TILE, (n + 1) * TILE)

            def one(s, carry):
                left = act[lhs, pl.ds(pl.multiple_of(s * SEQ, SEQ), SEQ), :]
                prod = jnp.dot(left, wt[n % 2].reshape(D, TILE), preferred_element_type=jnp.float32)
                acc[s, :SEQ, cols] = jnp.where(role == 4, acc[s, :SEQ, cols], 0.0) + prod
                return carry

            lax.fori_loop(s0, s1, one, 0)

        def epilogue(s, carry):
            @pl.when(role == 0)
            def _():
                norm_rope(la, 0, 1, s)

            @pl.when(role == 1)
            def _():
                norm_rope(la, 1, 2, s)

            @pl.when(role == 2)
            def _():
                def body(r0):
                    act[3, act_rows(s, r0), :] = acc[s, pl.ds(r0, RB), :].astype(jnp.bfloat16)

                rows(body)

            @pl.when(role == 3)
            def _():
                gain = gain_row(la, 2)

                def body(r0):
                    h = act[0, act_rows(s, r0), :].astype(jnp.float32) + scaled(acc[s, pl.ds(r0, RB), :], gain)
                    h2[la, s, pl.ds(r0, RB), :] = h.astype(jnp.bfloat16)

                rows(body)

            return carry

        lax.fori_loop(s0, s1, epilogue, 0)

    def swiglu(prod):
        gate = prod[:, :BLK].astype(jnp.bfloat16).astype(jnp.float32)
        up = prod[:, BLK:].astype(jnp.bfloat16).astype(jnp.float32)
        return (jax.nn.silu(gate) * up).astype(jnp.bfloat16)

    def shared_mlp(i, hn, la, j, s):
        def col(n):
            return 4096 * (n // 2) + 2048 * xx + 1024 * (n % 2) + BLK * j

        load_gu(i, la, col, 0)
        for n in range(N_TILE):
            if n + 1 < N_TILE:
                load_gu(i, la, col, n + 1)
            else:
                load_dn(hn, la, j, 0)
            wait_tile(n)
            prod = jnp.dot(h2[la, s], wt[n % 2].reshape(D, TILE), preferred_element_type=jnp.float32)
            mj[:, n * BLK:(n + 1) * BLK] = swiglu(prod)
        for n in range(N_TILE):
            if n + 1 < N_TILE:
                load_dn(hn, la, j, n + 1)
            wait_tile(n, 4)
            cols = slice(n * TILE, (n + 1) * TILE)
            prod = jnp.dot(mj[...], wt[n % 2, :4].reshape(4 * BLK, TILE), preferred_element_type=jnp.float32)
            acc[s, :, cols] = jnp.where(j > 0, acc[s, :, cols], 0.0) + prod

    def plain_gu(i, e):
        def col(n):
            return 1024 * (4 * e + n) + 3 * BLK

        load_gu(i, 1, col, 0)
        for n in range(N_TILE):
            if n + 1 < N_TILE:
                load_gu(i, 1, col, n + 1)
            wait_tile(n)

            def one(s, carry):
                prod = jnp.dot(h2[1, s, :SEQ], wt[n % 2].reshape(D, TILE), preferred_element_type=jnp.float32)
                act[4, pl.ds(pl.multiple_of(s * SEQ, SEQ), SEQ), pl.ds(m256(e * 1024 + n * BLK), BLK)] = swiglu(prod)
                return carry

            lax.fori_loop(0, 2, one, 0)

    def finish(la, s):
        gain = gain_row(la, 3)

        def body(r0):
            y = scaled(acc[s, pl.ds(r0, RB), :] + rs[la, s, pl.ds(r0, RB), :], gain)
            act[0, act_rows(s, r0), :] = (h2[la, s, pl.ds(r0, RB), :].astype(jnp.float32) + y).astype(jnp.bfloat16)

        rows(body)

    def pick(p, values):
        out = jnp.int32(0)
        for k, v in enumerate(values):
            if v:
                out = jnp.where(p == k, v, out)
        return out

    gain_copies = []
    for k in range(1, N_BLK):
        cp = pltpu.make_async_remote_copy(gain_ref, gains.at[me], gs_sem.at[k], gr_sem.at[k], device_id=(zz, (me + k) % N_BLK), device_id_type=MESH)
        gain_copies.append(cp)

    types = ['mm', 'at', 'h', 'wgu', 'wd', 'fin']

    def step(p, carry):
        for k in range(n_slot):
            if not lists[k]:
                continue

            @pl.when(p == k)
            def _(k=k):
                if k == 0:
                    for cp in gain_copies:
                        cp.start()
                for op in lists[k]:
                    transfer(op)
                if k == 0:
                    x_copy.wait()
                    for cp in gain_copies:
                        cp.wait()
                    gains[pl.ds(me, 1)] = gain_ref[...][None]

        ty = pick(p, [types.index(o[0]) for o in order])
        item = pick(p, [o[1] for o in order])
        la = pick(p, [o[2] for o in order])
        ex = pick(p, [o[3] for o in order])
        hf = pick(p, [o[4] for o in order])
        hn = pick(p, [H_ITEMS.index(o[1]) if o[0] == 'h' else 0 for o in order])
        pl.when((ty == 0) | (ty == 4))(lambda: mm(item, la, ex, hf))
        pl.when(ty == 1)(lambda: attention(ex, hf))
        pl.when(ty == 2)(lambda: shared_mlp(item, hn, la, ex, hf))
        pl.when(ty == 3)(lambda: plain_gu(item, ex))
        pl.when(ty == 5)(lambda: finish(la, hf))
        return carry

    lax.fori_loop(0, n_slot, step, 0)

    out_copy = pltpu.make_async_copy(act.at[0], out_hbm, io_sem)
    out_copy.start()
    drained = [op[1] for ops in lists for op in ops if op[0] == 'drain']
    for key, _ in KEYS:
        if key not in drained:
            same_size(key).wait_send()
    out_copy.wait()


def solution(mesh):
    cos_np, sin_np = rope_tables()
    hbm = pl.BlockSpec(memory_space=pl.ANY)
    vmem = pl.BlockSpec(memory_space=pltpu.VMEM)
    n_copy = len(KEYS)

    def local_fn(tokens, weights, gain_vecs):
        gains = jnp.stack(gain_vecs, axis=1).reshape(8, BLK).astype(jnp.float32)
        flat = tokens.reshape(ROWS, D)
        out = pl.pallas_call(
            kernel,
            out_shape=(
                jax.ShapeDtypeStruct((ROWS, D), jnp.bfloat16),
                jax.ShapeDtypeStruct((len(ITEMS), N_BLK, BLK, D), jnp.bfloat16),
                jax.ShapeDtypeStruct((len(H_ITEMS), 4, BLK, D), jnp.bfloat16),
            ),
            in_specs=[hbm, vmem, vmem, vmem] + [hbm] * 7,
            out_specs=(hbm, hbm, hbm),
            scratch_shapes=[
                pltpu.VMEM((5, ROWS, D), jnp.bfloat16),
                pltpu.VMEM((2, 2, 2 * SEQ, D), jnp.bfloat16),
                pltpu.VMEM((2 * SEQ, 4 * BLK), jnp.bfloat16),
                pltpu.VMEM((2, 2 * SEQ, D), jnp.float32),
                pltpu.VMEM((2, 2, SEQ, D), jnp.float32),
                pltpu.VMEM((2, N_BLK, BLK, TILE), jnp.bfloat16),
                pltpu.VMEM((N_BLK, 8, BLK), jnp.float32),
                pltpu.SemaphoreType.DMA((n_copy,)),
                pltpu.SemaphoreType.DMA((n_copy,)),
                pltpu.SemaphoreType.DMA((2,)),
                pltpu.SemaphoreType.DMA((N_BLK,)),
                pltpu.SemaphoreType.DMA((N_BLK,)),
                pltpu.SemaphoreType.DMA,
            ],
            compiler_params=pltpu.CompilerParams(collective_id=0, has_side_effects=True, vmem_limit_bytes=60 * 1024 * 1024),
        )(flat, jnp.asarray(cos_np), jnp.asarray(sin_np), gains, *weights)
        return out[0].reshape(tokens.shape)

    mapped = jax.shard_map(local_fn, mesh=mesh, in_specs=(P(('dp', 'fsdp')), P(None, 'fsdp'), P(None, 'fsdp')), out_specs=P(('dp', 'fsdp')), check_vma=False)

    def run(tokens, w_query, w_key, w_value, w_out, w_gate, w_up, w_down, g_query, g_key, g_attn, g_mlp):
        return mapped(tokens, (w_query, w_key, w_value, w_out, w_gate, w_up, w_down), (g_query, g_key, g_attn, g_mlp))

    return run
```

time: 1420 us -> 604 us (0.43)
  waiting for transfers between devices: 1010 us -> 0 us
  Pallas kernels: 0 us -> 595 us
  matrix products: 228 us -> 0 us
  blocking collectives: 70.4 us -> 0 us
  local copies, waits for them, and re-layouts: 59.9 us -> 6.5 us
  other arithmetic: 28.4 us -> 0.02 us
    all_gather x14 -> x0, waiting for transfers between devices: 1010 us -> none  [gather_rows(): return lax.all_gather(arr_w[layer_idx], 'fsdp', axis=0, tiled=True)]
    pallas_call x0 -> x1, Pallas kernels: none -> 595 us  [local_fn(): pl.pallas_call(kernel, out_shape=(jax.ShapeDtypeStruct((ROWS, D), jnp.bfl...]
    dot_general x18 -> x0, matrix products: 228 us -> none  [the longest x14 218 us: dot_bf16(): jnp.dot(left, right, preferred_element_type=jnp.float32)]
    all_gather x8 -> x0, blocking collectives: 70.4 us -> none  [gather_rows(): return lax.all_gather(arr_w[layer_idx], 'fsdp', axis=0, tiled=True)]
    slice x14 -> x0, local copies, waits for them, and re-layouts: 34.4 us -> none  [the longest x11 27.6 us: gather_rows(): return lax.all_gather(arr_w[layer_idx], 'fsdp', axis=0, tiled=True)]
    unnamed x64 -> x1, local copies, waits for them, and re-layouts: 18.6 us -> 3.16 us
  transfers between devices with their start and end apart: 14 -> 0, of which waited for: 12 -> 0; matrix products, arithmetic and copies ran while one was open for 20% -> 0% of each run, Pallas kernels for 0% -> 0%
where the time goes in v2:
time: 604 us; the launch traced here: 602 us
  Pallas kernels  595 us (99%)
  local copies, waits for them, and re-layouts  6.5 us (1%)
    pallas_call x1, Pallas kernels, local_fn(): pl.pallas_call(kernel, out_shape=(jax.ShapeDtypeStruct((ROWS, D), jnp.bfl...  595 us

profile of v2, /device:TPU:0, one launch (start us, length us, event | category | flops | bytes accessed | tf_op | source)
XLA Modules:
  0.0 602.0 jit_solution(8804872851813032500)
XLA Ops:
  0.0 0.7 copy.16
  0.7 0.7 copy.17
  1.4 0.7 copy.18
  2.0 0.7 copy.19
  2.7 0.6 reshape.11.gain_ref
  3.4 595.4 %shard_map.136 = (bf16[512,2048]{1,0:T(8,128)(2,1)}, bf16[18,8,256,2048]{3,2,1,0:T(8,128)(2,1)}, bf16[7,4,256,2048]{3,2,1,0:T(8,128)(2,1)}) custom-call(bf16[512,2048]{1,0:T(8,128)(2,1)} %bitcast.6, f32[256,128]{1,0:T(8,128)} %constant.4.clone.cos_ref, f32[256,128]{1,0:T(8,128)} %constant.5.clone.sin_ref, f32[8,256]{1,0:T(8,128)} %reshape.11.gain_ref, ...), custom_call_target="tpu_custom_call" | custom-call | tf_op jit(solution)/shard_map/pallas_call | solution.py:661
  598.8 3.2 copy.21
  (1 shorter events, 0.0 us)

commit v3 on v2

--- a/solution.py
+++ b/solution.py
@@ -24,47 +24,51 @@
 UNIT = 22.5 / 256
 LAT = 2.5
 PAIR = 4.0
-FLOW = {'A': (160, 128, 80, 48, 0), 'B': (128, 192, 0, 128, 0), 'H': (256, 128, 0, 128, 160), 'G': (224, 176, 0, 128, 192)}
-ITEMS = ['A'] * 4 + ['H'] * 4 + ['B'] * 4 + ['G'] * 3 + ['B'] * 3
+AXES = {'A': 'xy', 'B': 'xy', 'C': 'xy', 'H': 'xy', 'G': 'xy'}
+FLOW = {'A': (208, 144, 96, 48, 0), 'B': (128, 160, 0, 128, 0), 'C': (144, 192, 0, 144, 0), 'H': (208, 176, 0, 144, 128), 'G': (160, 144, 0, 128, 192)}
+ITEMS = ['A'] * 4 + ['H'] * 4 + ['B'] * 4 + ['G'] * 3 + ['C'] * 3
+BACKLOG = 18.0
 N_H = (4, 3)
-BACKLOG = 18.0
-COST = {'mm': 5.0, 'at': 7.0, 'h': 12.0, 'wgu': 9.0, 'wd': 9.0, 'fin': 3.0}
-
-
-def slots(nh=(4, 3)):
+COST = {'mm': 6.6, 'at': 4.5, 'h': 10.5, 'wgu': 7.5, 'wd': 11.0, 'fin': 1.5}
+BOTH = {'mm': 11.0, 'h': 11.6, 'wgu': 7.5, 'wd': 11.0}
+
+
+def slots(nh=N_H):
     out = []
     for k in range(3):
         out.append(('mm', k, 0, k, 2))
-    base = 4
     attn = (0, 4 + nh[0])
-    for la in range(2):
+    for s in range(2):
+        for q in range(2):
+            out.append(('at', 0, 0, q, s))
+        out.append(('mm', 3, 0, 3, s))
+    for j in range(nh[0]):
         for s in range(2):
-            if la:
-                for k in range(3):
-                    out.append(('mm', attn[1] + k, 1, k, s))
-            for q in range(2):
-                out.append(('at', 0, la, q, s))
-            out.append(('mm', attn[la] + 3, la, 3, s))
-        h0 = attn[la] + 4
-        if la == 0:
-            for j in range(nh[0]):
-                for s in range(2):
-                    out.append(('h', h0 + j, 0, j, s))
-        else:
-            for s in range(2):
-                for j in range(nh[1]):
-                    out.append(('h', h0 + j, 1, j, s))
-            w0 = h0 + nh[1]
-            if nh[1] < 4:
-                out.append(('wgu', w0, 1, 0, 2))
-                out.append(('wgu', w0 + 1, 1, 1, 2))
-                out.append(('wd', w0 + 2, 1, 4, 2))
-        for s in range(2):
-            out.append(('fin', 0, la, 0, s))
+            out.append(('h', 4 + j, 0, j, s))
+    for s in range(2):
+        out.append(('fin', 0, 0, 0, s))
+    a1 = attn[1]
+    h0 = a1 + 4
+    for s in range(2):
+        for k in range(3):
+            out.append(('mm', a1 + k, 1, k, s))
+        for q in range(2):
+            out.append(('at', 0, 1, q, s))
+        out.append(('mm', a1 + 3, 1, 3, s))
+    for s in range(2):
+        for j in range(nh[1]):
+            out.append(('h', h0 + j, 1, j, s))
+    w0 = h0 + nh[1]
+    if nh[1] < 4:
+        out.append(('wgu', w0, 1, 0, 2))
+        out.append(('wgu', w0 + 1, 1, 1, 2))
+        out.append(('wd', w0 + 2, 1, 4, 2))
+    for s in range(2):
+        out.append(('fin', 0, 1, 0, s))
     return out
 
 
-def schedule(thr=20.0, nh=(4, 3)):
+def schedule(thr=20.0, nh=N_H):
     sl = slots(nh)
     t = 0.0
     free = dict(x=0.0, y=0.0, z=0.0, p=0.0)
@@ -78,61 +82,36 @@
         busy[link] += dur
         arr[key] = free[link] + LAT
 
-    xq = [i for i in range(len(ITEMS))]
-    yq = []
-    for i, f in enumerate(ITEMS):
-        yq.append(('oy', i))
-        if f in 'HG':
-            yq.append(('on', i))
-    pend = []
+    todo_send = {}
     for i, f in enumerate(ITEMS):
         px, py, dx, dy, pn = FLOW[f]
-        pend.append((('fx', i), [('X', i)]))
-        pend.append((('fy', i), [('Y', i)]))
-        pend.append((('fd', i), ([('DX', i)] if dx else []) + [('DY', i)]))
+        a, b = AXES[f]
+
+        def add(k, link, dur, *deps):
+            todo_send[(k, i)] = (i, link, dur, [(d, i) for d in deps])
+
+        add('X', a, px * UNIT)
+        add('Y', b, py * UNIT)
+        add('P0', 'p', PAIR)
+        add('DY', b, dy * UNIT, 'X')
+        if dx:
+            add('DX', a, dx * UNIT, 'Y')
         if px < 256:
-            pend.append((('px', i), [('X', i), ('ZX', i)]))
-        pend.append((('py', i), [('Y', i), ('ZY', i)]))
-        pend.append((('pd', i), ([('DX', i)] if dx else []) + [('DY', i), ('ZD', i)]))
+            add('ZX', 'z', (256 - px) * UNIT, 'X')
+            add('P1', 'p', PAIR, 'X', 'ZX')
+        else:
+            add('P1', 'p', PAIR, 'X')
+        add('ZY', 'z', (256 - py) * UNIT, 'Y')
+        add('P2', 'p', PAIR, 'Y', 'ZY')
+        diag = ('DX', 'DY') if dx else ('DY',)
+        add('ZD', 'z', (256 - dx - dy) * UNIT, *diag)
+        add('P3', 'p', PAIR, *(diag + ('ZD',)))
         if pn:
-            pend.append((('fn', i), [('N', i)]))
-            pend.append((('pn', i), [('N', i), ('ZN', i)]))
-
-    def run(op):
-        if op[0] in ('ag', 'rs'):
-            units, key = (1, 'H') if op[0] == 'ag' else (2, 'R')
-            send('x', units * 22.5, (key,) + op[1:])
-            prog.append(op)
-            return
-        kind, i = op
-        px, py, dx, dy, pn = FLOW[ITEMS[i]]
-        if kind == 'ox':
-            send('x', px * UNIT, ('X', i))
-        elif kind == 'oy':
-            send('y', py * UNIT, ('Y', i))
-            send('p', PAIR, ('P0', i))
-        elif kind == 'on':
-            send('y', pn * UNIT, ('N', i))
-            send('p', PAIR, ('Q0', i))
-        elif kind == 'fx':
-            if px < 256:
-                send('z', (256 - px) * UNIT, ('ZX', i))
-            else:
-                send('p', PAIR, ('P1', i))
-            send('y', dy * UNIT, ('DY', i))
-        elif kind == 'fy':
-            send('z', (256 - py) * UNIT, ('ZY', i))
-            if dx:
-                send('x', dx * UNIT, ('DX', i))
-        elif kind == 'fd':
-            send('z', (256 - dx - dy) * UNIT, ('ZD', i))
-        elif kind == 'fn':
-            send('z', (256 - pn) * UNIT, ('ZN', i))
-        elif kind in ('px', 'py', 'pd'):
-            send('p', PAIR, (dict(px='P1', py='P2', pd='P3')[kind], i))
-        elif kind == 'pn':
-            send('p', PAIR, ('Q1', i))
-        prog.append(op)
+            add('N', b, pn * UNIT)
+            add('Q0', 'p', PAIR)
+            add('ZN', 'z', (256 - pn) * UNIT, 'N')
+            add('Q1', 'p', PAIR, 'N', 'ZN')
+    limit = dict(x=thr, y=thr, z=thr, p=2 * PAIR)
 
     def needs(s):
         ty, it, la, ex, hf = s
@@ -148,6 +127,7 @@
 
     def after(s):
         ty, it, la, ex, hf = s
+        halves = [hf] if hf < 2 else [0, 1]
         if ty == 'mm' and ex < 3:
             return [('fin', la - 1, 0, hf)] if la else []
         if ty == 'at':
@@ -155,7 +135,7 @@
         if ty == 'mm':
             return [('at', la, q, hf) for q in range(2)]
         if ty == 'h':
-            return [('mm', la, 3, hf)] + ([('h', la, ex - 1, hf)] if ex else [])
+            return [('mm', la, 3, q) for q in halves] + ([('h', la, ex - 1, hf)] if ex else [])
         if ty == 'wgu':
             return [('mm', la, 3, 0), ('mm', la, 3, 1)]
         if ty == 'wd':
@@ -168,19 +148,18 @@
         again = True
         while again:
             again = False
-            for op, ns in list(pend):
-                if all(arr.get(x, 1e9) <= t for x in ns):
-                    pend.remove((op, ns))
-                    run(op)
-                    again = True
-            if xq and free['x'] - t < thr:
-                run(('ox', xq.pop(0)))
-                again = True
-            if yq and free['y'] - t < thr:
-                run(yq.pop(0))
+            ready = {}
+            for key, (pri, link, dur, deps) in todo_send.items():
+                if free[link] - t < limit[link] and all(arr.get(x, 1e9) <= t for x in deps):
+                    if link not in ready or (pri, len(deps) == 0) < ready[link][0]:
+                        ready[link] = ((pri, len(deps) == 0), key)
+            for link, (_, key) in ready.items():
+                send(link, todo_send[key][2], key)
+                prog.append(('send', key, todo_send.pop(key)[3]))
                 again = True
         pick = None
-        ev = [arr[x] for op, n2 in pend for x in n2 if x in arr]
+        ev = [arr[x] for e in todo_send.values() for x in e[3] if x in arr]
+        ev += [free[e[1]] - limit[e[1]] + 0.01 for e in todo_send.values()]
         for k in todo:
             s = sl[k]
             if not all(x in done for x in after(s)):
@@ -194,48 +173,53 @@
             s = sl[pick]
             todo.remove(pick)
             prog.append(('slot', pick))
-            t += COST[s[0]] * (2 if s[0] == 'mm' and s[4] == 2 else 1)
+            t += BOTH[s[0]] if s[4] == 2 else COST[s[0]]
             done.add((s[0], s[2], s[3], s[4]))
-            if s[0] == 'mm' and s[3] == 3:
-                run(('ag', s[2], s[4]))
-            if s[0] == 'h' and s[3] == nh[s[2]] - 1:
-                run(('rs', s[2], s[4]))
+            halves = [s[4]] if s[4] < 2 else [0, 1]
+            for q in halves:
+                key = None
+                if s[0] == 'mm' and s[3] == 3:
+                    key, units = ('H', s[2], q), 1
+                if s[0] == 'h' and s[3] == nh[s[2]] - 1:
+                    key, units = ('R', s[2], q), 2
+                if key:
+                    todo_send[key] = (-1, AXES['HG'[s[2]]][0], units * 22.5, [])
             continue
-        if xq:
-            ev.append(free['x'] - thr + 0.01)
-        if yq:
-            ev.append(free['y'] - thr + 0.01)
         t = min(e for e in ev if e > t)
-    assert not pend and not xq and not yq
+    assert not todo_send
     return sl, prog, t
 
 
 def plan():
     sl, prog, _ = schedule(BACKLOG, N_H)
     order, lists, cur, seen = [], [], [], set()
+
+    def await_all(keys):
+        for key in keys:
+            if key not in seen:
+                seen.add(key)
+                cur.append(('wait', key))
+
     for op in prog:
-        if op[0] != 'slot':
-            cur.append(op)
+        if op[0] == 'send':
+            await_all(op[2])
+            cur.append(('send', op[1]))
             continue
         s = sl[op[1]]
         ty, it, la, ex, hf = s
-        need = []
         if ty in ('mm', 'h', 'wgu', 'wd'):
-            need += [('P%d' % k, it) for k in range(4)]
+            await_all([('P%d' % k, it) for k in range(4)])
         if ty == 'h':
-            need += [('Q%d' % k, it) for k in range(2)] + [('H', la, hf)]
+            await_all([('Q%d' % k, it) for k in range(2)])
+            await_all([('H', la, hf)])
             if la == 1 and ex == 0:
                 cur.append(('drain', ('R', 0, hf)))
         if ty == 'fin':
-            need.append(('R', la, hf))
-        for key in need:
-            if key not in seen:
-                seen.add(key)
-                cur.append(('wait', key))
+            await_all([('R', la, hf)])
         order.append(s)
         lists.append(cur)
         cur = []
-    assert not cur or all(op[0] in ('ag', 'rs') for op in cur)
+    assert not cur and all(k in seen for k, _ in KEYS)
     return order, lists
 
 
@@ -269,7 +253,7 @@
     return (np.concatenate([cos, cos], 1).astype(np.float32), np.concatenate([-sin, sin], 1).astype(np.float32))
 
 
-def kernel(x_hbm, cos_ref, sin_ref, gain_ref, wq, wk, wv, wo, wg, wu, wd, out_hbm, full, full_n, act, h2, mj, acc, rs, wt, gains, send_sem, recv_sem, wt_sem, gs_sem, gr_sem, io_sem):
+def kernel(x_hbm, cos_ref, sin_ref, gq, gk, ga, gm, wq, wk, wv, wo, wg, wu, wd, out_hbm, full, full_n, act, h2, mj, acc, rs, wt, gains, gain_in, gain_ref, send_sem, recv_sem, wt_sem, gs_sem, gr_sem, io_sem, gi_sem):
     zz = lax.axis_index('dp')
     me = lax.axis_index('fsdp')
     cc = me % 2
@@ -288,6 +272,14 @@
 
     x_copy = pltpu.make_async_copy(x_hbm, act.at[0], io_sem)
     x_copy.start()
+
+    gain_loads = [pltpu.make_async_copy(g, gain_in.at[k], gi_sem.at[k]) for k, g in enumerate((gq, gk, ga, gm))]
+    for cp in gain_loads:
+        cp.start()
+    for k, cp in enumerate(gain_loads):
+        cp.wait()
+        for la in range(2):
+            gain_ref[la * 4 + k:la * 4 + k + 1, :] = gain_in[k, la:la + 1, :].astype(jnp.float32)
 
     barrier = pltpu.get_barrier_semaphore()
     for k in range(1, N_BLK):
@@ -328,80 +320,60 @@
             out.append((wu.at[la, :, pl.ds(c, BLK)], n * TILE + BLK, BLK))
         return out
 
-    def send_own(key, i, side, off, rows, dev):
-        part = pl.ds(off, rows)
+    def send_own(key, side, off, dev):
+        i = key[1]
+        part = pl.ds(off, KROWS[key])
         for src, c0, nc in own_pieces(i, side):
             remote(key, src.at[part, :], full.at[i, me, part, pl.ds(c0, nc)], dev).start()
 
-    def push(key, i, blk, off, dev):
-        piece = full.at[i, blk, pl.ds(off, KROWS[key]), :]
+    def push(key, blk, off, dev):
+        piece = full.at[key[1], blk, pl.ds(off, KROWS[key]), :]
         remote(key, piece, piece, dev).start()
 
-    def push_n(key, i, off, dev):
-        piece = full_n.at[H_ITEMS.index(i), n_y, pl.ds(off, KROWS[key]), :]
+    def push_n(key, off, dev):
+        piece = full_n.at[H_ITEMS.index(key[1]), n_y, pl.ds(off, KROWS[key]), :]
         remote(key, piece, piece, dev).start()
 
+    def own_n(key, off, dev):
+        i = key[1]
+        la = int(i >= ATTN0[1])
+        r0 = BLK * (i - ATTN0[la] - 4)
+        rr = KROWS[key]
+        remote(key, wd.at[la, pl.ds(m16(r0 + off), rr), :], full_n.at[H_ITEMS.index(i), n_me, pl.ds(off, rr), :], dev).start()
+
     def transfer(op):
-        kind = op[0]
-        if kind == 'wait':
-            arrived(op[1])
-        elif kind == 'drain':
-            same_size(op[1]).wait_send()
-        elif kind == 'ag':
-            la, s = op[1:]
-            remote(('H', la, s), h2.at[la, s, pl.ds(0, SEQ), :], h2.at[la, s, pl.ds(SEQ, SEQ), :], dev_x).start()
-        elif kind == 'rs':
-            la, s = op[1:]
-            remote(('R', la, s), acc.at[s, pl.ds(SEQ, SEQ), :], rs.at[la, s], dev_x).start()
-        else:
-            i = op[1]
-            px, py, dx, dy, pn = FLOW[ITEMS[i]]
-            off_d = m16((BLK - dx - dy) * zz)
-            if kind == 'ox':
-                send_own(('X', i), i, 1 - xx, m16((BLK - px) * zz), px, dev_x)
-            elif kind == 'oy':
-                send_own(('Y', i), i, xx, m16((BLK - py) * zz), py, dev_y)
-                send_own(('P0', i), i, xx, 0, BLK, dev_p)
-            elif kind == 'fx':
-                arrived(('X', i))
-                if px < BLK:
-                    push(('ZX', i), i, f_x, m16(px * zz), dev_z)
-                else:
-                    push(('P1', i), i, f_x, 0, dev_p)
-                push(('DY', i), i, f_x, m16(off_d + dx), dev_y)
-            elif kind == 'fy':
-                arrived(('Y', i))
-                push(('ZY', i), i, f_y, m16(py * zz), dev_z)
-                if dx:
-                    push(('DX', i), i, f_y, off_d, dev_x)
-            elif kind == 'fd':
-                if dx:
-                    arrived(('DX', i))
-                arrived(('DY', i))
-                push(('ZD', i), i, f_d, m16((dx + dy) * zz), dev_z)
-            elif kind == 'px':
-                arrived(('ZX', i))
-                push(('P1', i), i, f_x, 0, dev_p)
-            elif kind == 'py':
-                arrived(('ZY', i))
-                push(('P2', i), i, f_y, 0, dev_p)
-            elif kind == 'pd':
-                arrived(('ZD', i))
-                push(('P3', i), i, f_d, 0, dev_p)
-            else:
-                hn = H_ITEMS.index(i)
-                la = int(i >= ATTN0[1])
-                r0 = BLK * (i - ATTN0[la] - 4)
-                if kind == 'on':
-                    off = m16((BLK - pn) * zz)
-                    remote(('N', i), wd.at[la, pl.ds(m16(r0 + off), pn), :], full_n.at[hn, n_me, pl.ds(off, pn), :], dev_y).start()
-                    remote(('Q0', i), wd.at[la, pl.ds(r0, BLK), :], full_n.at[hn, n_me], dev_p).start()
-                elif kind == 'fn':
-                    arrived(('N', i))
-                    push_n(('ZN', i), i, m16(pn * zz), dev_z)
-                elif kind == 'pn':
-                    arrived(('ZN', i))
-                    push_n(('Q1', i), i, 0, dev_p)
+        key = op[1]
+        if op[0] == 'wait':
+            return arrived(key)
+        if op[0] == 'drain':
+            return same_size(key).wait_send()
+        kind = key[0]
+        if kind == 'H':
+            la, s = key[1:]
+            return remote(key, h2.at[la, s, pl.ds(0, SEQ), :], h2.at[la, s, pl.ds(SEQ, SEQ), :], dev_x).start()
+        if kind == 'R':
+            la, s = key[1:]
+            return remote(key, acc.at[s, pl.ds(SEQ, SEQ), :], rs.at[la, s], dev_x).start()
+        px, py, dx, dy, pn = FLOW[ITEMS[key[1]]]
+        off_d = m16((BLK - dx - dy) * zz)
+        steps = {
+            'X': lambda: send_own(key, 1 - xx, m16((BLK - px) * zz), dev_x),
+            'Y': lambda: send_own(key, xx, m16((BLK - py) * zz), dev_y),
+            'P0': lambda: send_own(key, xx, 0, dev_p),
+            'ZX': lambda: push(key, f_x, m16(px * zz), dev_z),
+            'ZY': lambda: push(key, f_y, m16(py * zz), dev_z),
+            'ZD': lambda: push(key, f_d, m16((dx + dy) * zz), dev_z),
+            'DX': lambda: push(key, f_y, off_d, dev_x),
+            'DY': lambda: push(key, f_x, m16(off_d + dx), dev_y),
+            'P1': lambda: push(key, f_x, 0, dev_p),
+            'P2': lambda: push(key, f_y, 0, dev_p),
+            'P3': lambda: push(key, f_d, 0, dev_p),
+            'N': lambda: own_n(key, m16((BLK - pn) * zz), dev_y),
+            'Q0': lambda: own_n(key, 0, dev_p),
+            'ZN': lambda: push_n(key, m16(pn * zz), dev_z),
+            'Q1': lambda: push_n(key, 0, dev_p),
+        }
+        steps[kind]()
 
     order, lists = plan()
     n_slot = len(order)
@@ -545,6 +517,9 @@
         gate = prod[:, :BLK].astype(jnp.bfloat16).astype(jnp.float32)
         up = prod[:, BLK:].astype(jnp.bfloat16).astype(jnp.float32)
         return (jax.nn.silu(gate) * up).astype(jnp.bfloat16)
+
+    def halves(hf):
+        return jnp.where(hf == 2, 0, hf), jnp.where(hf == 2, 2, hf + 1)
 
     def shared_mlp(i, hn, la, j, s):
         def col(n):
@@ -656,7 +631,6 @@
     n_copy = len(KEYS)
 
     def local_fn(tokens, weights, gain_vecs):
-        gains = jnp.stack(gain_vecs, axis=1).reshape(8, BLK).astype(jnp.float32)
         flat = tokens.reshape(ROWS, D)
         out = pl.pallas_call(
             kernel,
@@ -665,7 +639,7 @@
                 jax.ShapeDtypeStruct((len(ITEMS), N_BLK, BLK, D), jnp.bfloat16),
                 jax.ShapeDtypeStruct((len(H_ITEMS), 4, BLK, D), jnp.bfloat16),
             ),
-            in_specs=[hbm, vmem, vmem, vmem] + [hbm] * 7,
+            in_specs=[hbm, vmem, vmem] + [hbm] * 11,
             out_specs=(hbm, hbm, hbm),
             scratch_shapes=[
                 pltpu.VMEM((5, ROWS, D), jnp.bfloat16),
@@ -675,15 +649,18 @@
                 pltpu.VMEM((2, 2, SEQ, D), jnp.float32),
                 pltpu.VMEM((2, N_BLK, BLK, TILE), jnp.bfloat16),
                 pltpu.VMEM((N_BLK, 8, BLK), jnp.float32),
+                pltpu.VMEM((4, 2, BLK), jnp.bfloat16),
+                pltpu.VMEM((8, BLK), jnp.float32),
                 pltpu.SemaphoreType.DMA((n_copy,)),
                 pltpu.SemaphoreType.DMA((n_copy,)),
                 pltpu.SemaphoreType.DMA((2,)),
                 pltpu.SemaphoreType.DMA((N_BLK,)),
                 pltpu.SemaphoreType.DMA((N_BLK,)),
                 pltpu.SemaphoreType.DMA,
+                pltpu.SemaphoreType.DMA((4,)),
             ],
             compiler_params=pltpu.CompilerParams(collective_id=0, has_side_effects=True, vmem_limit_bytes=60 * 1024 * 1024),
-        )(flat, jnp.asarray(cos_np), jnp.asarray(sin_np), gains, *weights)
+        )(flat, jnp.asarray(cos_np), jnp.asarray(sin_np), *gain_vecs, *weights)
         return out[0].reshape(tokens.shape)
 
     mapped = jax.shard_map(local_fn, mesh=mesh, in_specs=(P(('dp', 'fsdp')), P(None, 'fsdp'), P(None, 'fsdp')), out_specs=P(('dp', 'fsdp')), check_vma=False)

time: 604 us -> 595 us (0.985)
    pallas_call x1, Pallas kernels: 595 us -> 589 us  [local_fn(): pl.pallas_call(kernel, out_shape=(jax.ShapeDtypeStruct((ROWS, D), jnp.bfl...]
where the time goes in v3:
time: 595 us; the launch traced here: 592 us
  Pallas kernels  589 us (99%)
    pallas_call x1, Pallas kernels, local_fn(): pl.pallas_call(kernel, out_shape=(jax.ShapeDtypeStruct((ROWS, D), jnp.bfl...  589 us

profile of v3, /device:TPU:0, one launch (start us, length us, event | category | flops | bytes accessed | tf_op | source)
XLA Modules:
  0.0 592.3 jit_solution(9046297433591392380)
XLA Ops:
  0.0 589.2 %shard_map.136 = (bf16[512,2048]{1,0:T(8,128)(2,1)}, bf16[18,8,256,2048]{3,2,1,0:T(8,128)(2,1)}, bf16[7,4,256,2048]{3,2,1,0:T(8,128)(2,1)}) custom-call(bf16[512,2048]{1,0:T(8,128)(2,1)} %bitcast.2, f32[256,128]{1,0:T(8,128)} %constant.4.clone.cos_ref, f32[256,128]{1,0:T(8,128)} %constant.5.clone.sin_ref, bf16[2,256]{1,0:T(2,128)(2,1)} %gq.1, ...), custom_call_target="tpu_custom_call" | custom-call | tf_op jit(solution)/shard_map/pallas_call | solution.py:635
  589.2 3.2 copy.16

commit v4 on v3

--- a/solution.py
+++ b/solution.py
@@ -18,77 +18,86 @@
 BLK = 256
 TILE = 512
 N_TILE = D // TILE
+HALF = D // 2
 RB = 32
+SLOTS = 2
 MESH = pl.DeviceIdType.MESH
 
-UNIT = 22.5 / 256
+START = 0.0
+ONE_MIB = 22.5
+PAIRED = range(2)
+ROLES = range(3)
+QUAD = range(4)
+UNIT = ONE_MIB / 256
 LAT = 2.5
 PAIR = 4.0
-AXES = {'A': 'xy', 'B': 'xy', 'C': 'xy', 'H': 'xy', 'G': 'xy'}
-FLOW = {'A': (208, 144, 96, 48, 0), 'B': (128, 160, 0, 128, 0), 'C': (144, 192, 0, 144, 0), 'H': (208, 176, 0, 144, 128), 'G': (160, 144, 0, 128, 192)}
-ITEMS = ['A'] * 4 + ['H'] * 4 + ['B'] * 4 + ['G'] * 3 + ['C'] * 3
-BACKLOG = 18.0
+FLOW = {'A': (176, 144, 64), 'B': (144, 176, 144), 'C': (144, 176, 144), 'Q': (128, 128, 128), 'H': (144, 128, 128), 'G': (176, 144, 144)}
+VIA_X = {'A': 64}
+DOWN = {'H': 176, 'G': 208}
+FLOW = {k: (px, py, VIA_X.get(k, 0), dy, DOWN.get(k, 0)) for k, (px, py, dy) in FLOW.items()}
+ITEMS = ['Q'] * 3 + ['A'] + ['H'] * 4 + ['B'] * 4 + ['G'] * 3 + ['C'] * 3
+BACKLOG = 8.0
 N_H = (4, 3)
 COST = {'mm': 6.6, 'at': 4.5, 'h': 10.5, 'wgu': 7.5, 'wd': 11.0, 'fin': 1.5}
-BOTH = {'mm': 11.0, 'h': 11.6, 'wgu': 7.5, 'wd': 11.0}
+SCALE = {'Q': 0.5}
+BOTH = dict(COST, mq=11.0, mm=11.0, nr=3.0)
 
 
 def slots(nh=N_H):
     out = []
-    for k in range(3):
-        out.append(('mm', k, 0, k, 2))
+    for k in ROLES:
+        out.append(('mq', k, 0, k, 2))
+    for k in PAIRED:
+        out.append(('nr', 0, 0, k, 2))
     attn = (0, 4 + nh[0])
-    for s in range(2):
-        for q in range(2):
+    for s in PAIRED:
+        for q in (1, 0):
             out.append(('at', 0, 0, q, s))
         out.append(('mm', 3, 0, 3, s))
     for j in range(nh[0]):
-        for s in range(2):
+        for s in PAIRED:
             out.append(('h', 4 + j, 0, j, s))
-    for s in range(2):
+    for s in PAIRED:
         out.append(('fin', 0, 0, 0, s))
     a1 = attn[1]
     h0 = a1 + 4
-    for s in range(2):
-        for k in range(3):
+    for s in PAIRED:
+        for k in ROLES:
             out.append(('mm', a1 + k, 1, k, s))
-        for q in range(2):
+        for q in PAIRED:
             out.append(('at', 0, 1, q, s))
         out.append(('mm', a1 + 3, 1, 3, s))
-    for s in range(2):
+    for s in PAIRED:
         for j in range(nh[1]):
             out.append(('h', h0 + j, 1, j, s))
     w0 = h0 + nh[1]
-    if nh[1] < 4:
-        out.append(('wgu', w0, 1, 0, 2))
-        out.append(('wgu', w0 + 1, 1, 1, 2))
-        out.append(('wd', w0 + 2, 1, 4, 2))
-    for s in range(2):
+    out.append(('wgu', w0, 1, 0, 2))
+    out.append(('wgu', w0 + 1, 1, 1, 2))
+    out.append(('wd', w0 + 2, 1, 4, 2))
+    for s in PAIRED:
         out.append(('fin', 0, 1, 0, s))
     return out
 
 
 def schedule(thr=20.0, nh=N_H):
     sl = slots(nh)
-    t = 0.0
-    free = dict(x=0.0, y=0.0, z=0.0, p=0.0)
+    t = START
+    free = dict.fromkeys('xyzp', START)
     arr = {}
     prog = []
-    busy = dict(x=0.0, y=0.0, z=0.0, p=0.0)
 
     def send(link, dur, key):
         s = max(free[link], t)
         free[link] = s + dur
-        busy[link] += dur
         arr[key] = free[link] + LAT
 
     todo_send = {}
     for i, f in enumerate(ITEMS):
         px, py, dx, dy, pn = FLOW[f]
-        a, b = AXES[f]
-
-        def add(k, link, dur, *deps):
-            todo_send[(k, i)] = (i, link, dur, [(d, i) for d in deps])
+        a, b = 'xy'
+
+        def add(k, link, dur, *deps, i=i, f=f):
+            todo_send[(k, i)] = (i, link, dur * SCALE.get(f, 1.0), [(d, i) for d in deps])
 
         add('X', a, px * UNIT)
         add('Y', b, py * UNIT)
@@ -96,31 +105,39 @@
         add('DY', b, dy * UNIT, 'X')
         if dx:
             add('DX', a, dx * UNIT, 'Y')
-        if px < 256:
-            add('ZX', 'z', (256 - px) * UNIT, 'X')
+        if px < BLK:
+            add('ZX', 'z', (BLK - px) * UNIT, 'X')
             add('P1', 'p', PAIR, 'X', 'ZX')
         else:
             add('P1', 'p', PAIR, 'X')
-        add('ZY', 'z', (256 - py) * UNIT, 'Y')
+        add('ZY', 'z', (BLK - py) * UNIT, 'Y')
         add('P2', 'p', PAIR, 'Y', 'ZY')
         diag = ('DX', 'DY') if dx else ('DY',)
-        add('ZD', 'z', (256 - dx - dy) * UNIT, *diag)
+        add('ZD', 'z', (BLK - dx - dy) * UNIT, *diag)
         add('P3', 'p', PAIR, *(diag + ('ZD',)))
         if pn:
             add('N', b, pn * UNIT)
             add('Q0', 'p', PAIR)
-            add('ZN', 'z', (256 - pn) * UNIT, 'N')
+            add('ZN', 'z', (BLK - pn) * UNIT, 'N')
             add('Q1', 'p', PAIR, 'N', 'ZN')
+    for h in PAIRED:
+        todo_send[('T', 0, h)] = (-2, 'x', ONE_MIB, [])
     limit = dict(x=thr, y=thr, z=thr, p=2 * PAIR)
 
     def needs(s):
         ty, it, la, ex, hf = s
         n = []
-        if ty in ('mm', 'h', 'wgu', 'wd'):
-            n += [('P%d' % k, it) for k in range(4)]
+        if ty in ('mm', 'mq', 'h', 'wgu', 'wd'):
+            n += [('P%d' % k, it) for k in QUAD]
         if ty == 'h':
-            n += [('Q%d' % k, it) for k in range(2)]
+            n += [('Q%d' % k, it) for k in PAIRED]
             n.append(('H', la, hf))
+        if ty == 'mq':
+            n += [('T', 0, q) for q in PAIRED]
+        if ty == 'nr':
+            n.append(('S', 0, ex))
+        if ty == 'mm' and la == 0:
+            n.append(('O', 0, hf))
         if ty == 'fin':
             n.append(('R', la, hf))
         return n
@@ -130,17 +147,21 @@
         halves = [hf] if hf < 2 else [0, 1]
         if ty == 'mm' and ex < 3:
             return [('fin', la - 1, 0, hf)] if la else []
+        if ty == 'mq':
+            return [('nr', 0, ex - 1, 2)] if ex else []
+        if ty == 'nr':
+            return [('mq', 0, ex, 2)]
         if ty == 'at':
-            return [('mm', la, k, hf if la else 2) for k in range(3)]
+            return [('mm', la, k, hf) for k in ROLES] if la else [('mq', 0, 2, 2)] + [('nr', 0, k, 2) for k in PAIRED]
         if ty == 'mm':
-            return [('at', la, q, hf) for q in range(2)]
+            return [('at', la, q, hf) for q in PAIRED]
         if ty == 'h':
             return [('mm', la, 3, q) for q in halves] + ([('h', la, ex - 1, hf)] if ex else [])
         if ty == 'wgu':
-            return [('mm', la, 3, 0), ('mm', la, 3, 1)]
+            return [('mm', la, 3, q) for q in PAIRED]
         if ty == 'wd':
-            return [('wgu', la, 0, 2), ('wgu', la, 1, 2)] + [('h', la, nh[1] - 1, q) for q in range(2)]
-        return [('h', la, nh[la] - 1, hf)] + ([('wd', la, 4, 2)] if la and nh[1] < 4 else [])
+            return [('wgu', la, 0, 2), ('wgu', la, 1, 2)] + [('h', la, nh[1] - 1, q) for q in PAIRED]
+        return [('h', la, nh[la] - 1, hf)] + ([('wd', la, 4, 2)] if la else [])
 
     done = set()
     todo = list(range(len(sl)))
@@ -170,20 +191,23 @@
                 break
             ev += [arr[x] for x in ns if x in arr]
         if pick is not None:
-            s = sl[pick]
+            ty, it, la, ex, hf = sl[pick]
             todo.remove(pick)
             prog.append(('slot', pick))
-            t += BOTH[s[0]] if s[4] == 2 else COST[s[0]]
-            done.add((s[0], s[2], s[3], s[4]))
-            halves = [s[4]] if s[4] < 2 else [0, 1]
-            for q in halves:
+            t += BOTH[ty] if hf not in PAIRED else COST[ty]
+            done.add((ty, la, ex, hf))
+            for q in [hf] if hf in PAIRED else PAIRED:
                 key = None
-                if s[0] == 'mm' and s[3] == 3:
-                    key, units = ('H', s[2], q), 1
-                if s[0] == 'h' and s[3] == nh[s[2]] - 1:
-                    key, units = ('R', s[2], q), 2
+                if ty == 'mq' and ex in PAIRED and not q:
+                    key, units = ('S', 0, ex), 0.05
+                if ty == 'at' and not la and ex:
+                    key, units = ('O', 0, hf), 0.5
+                if ty == 'mm' and ex == 3:
+                    key, units = ('H', la, q), 1
+                if ty == 'h' and ex == nh[la] - 1:
+                    key, units = ('R', la, q), 2
                 if key:
-                    todo_send[key] = (-1, AXES['HG'[s[2]]][0], units * 22.5, [])
+                    todo_send[key] = (-1, 'x', units * ONE_MIB, [])
             continue
         t = min(e for e in ev if e > t)
     assert not todo_send
@@ -207,13 +231,21 @@
             continue
         s = sl[op[1]]
         ty, it, la, ex, hf = s
-        if ty in ('mm', 'h', 'wgu', 'wd'):
-            await_all([('P%d' % k, it) for k in range(4)])
+        if ty in ('mm', 'mq', 'h', 'wgu', 'wd'):
+            await_all([('P%d' % k, it) for k in QUAD])
         if ty == 'h':
-            await_all([('Q%d' % k, it) for k in range(2)])
+            await_all([('Q%d' % k, it) for k in PAIRED])
             await_all([('H', la, hf)])
             if la == 1 and ex == 0:
                 cur.append(('drain', ('R', 0, hf)))
+        if ty == 'mq':
+            await_all([('T', 0, q) for q in PAIRED])
+        if ty == 'nr':
+            await_all([('S', 0, ex)])
+        if ty == 'mm' and la == 0:
+            await_all([('O', 0, hf)])
+        if ty == 'mm' and la == 1 and ex == 0:
+            cur.append(('drain', ('O', 0, hf)))
         if ty == 'fin':
             await_all([('R', la, hf)])
         order.append(s)
@@ -231,8 +263,10 @@
         if pn:
             rows.update({'N': pn, 'ZN': BLK - pn, 'Q0': BLK, 'Q1': BLK})
         keys += [((k, i), r) for k, r in rows.items() if r]
-    for la in range(2):
-        for s in range(2):
+    for s in PAIRED:
+        keys += [(('T', 0, s), BLK), (('S', 0, s), 0), (('O', 0, s), BLK)]
+    for la in PAIRED:
+        for s in PAIRED:
             keys += [(('H', la, s), BLK), (('R', la, s), 0)]
     return keys
 
@@ -245,6 +279,26 @@
 W_ITEM = 8 + N_H[0] + N_H[1]
 
 
+def shared_col(n, side, j):
+    return 4096 * (n // 2) + 2048 * side + 1024 * (n % 2) + BLK * j
+
+
+def head(h):
+    return slice(h * HEAD_DIM, (h + 1) * HEAD_DIM)
+
+
+def tile(n):
+    return slice(n * TILE, (n + 1) * TILE)
+
+
+def seq(s):
+    return pl.ds(pl.multiple_of(s * SEQ, SEQ), SEQ)
+
+
+def loop(n, body):
+    lax.fori_loop(0, n, body, 0)
+
+
 def rope_tables():
     pos = np.arange(SEQ, dtype=np.float64)
     inv = THETA ** (-2.0 * np.arange(HEAD_DIM // 2, dtype=np.float64) / HEAD_DIM)
@@ -253,7 +307,12 @@
     return (np.concatenate([cos, cos], 1).astype(np.float32), np.concatenate([-sin, sin], 1).astype(np.float32))
 
 
-def kernel(x_hbm, cos_ref, sin_ref, gq, gk, ga, gm, wq, wk, wv, wo, wg, wu, wd, out_hbm, full, full_n, act, h2, mj, acc, rs, wt, gains, gain_in, gain_ref, send_sem, recv_sem, wt_sem, gs_sem, gr_sem, io_sem, gi_sem):
+def width(key):
+    narrow = key[0] == 'O' or (len(key) == 2 and ITEMS[key[1]] == 'Q')
+    return HALF if narrow else D
+
+
+def kernel(x_hbm, cos_ref, sin_ref, gq, gk, ga, gm, wq, wk, wv, wo, wg, wu, wd, out_hbm, full, full_n, act, h2, mj, acc, rs, xo, st_out, st_in, wt, gains, gain_in, gain_ref, send_sem, recv_sem, wt_sem, gs_sem, gr_sem, io_sem, gi_sem):
     zz = lax.axis_index('dp')
     me = lax.axis_index('fsdp')
     cc = me % 2
@@ -278,7 +337,7 @@
         cp.start()
     for k, cp in enumerate(gain_loads):
         cp.wait()
-        for la in range(2):
+        for la in PAIRED:
             gain_ref[la * 4 + k:la * 4 + k + 1, :] = gain_in[k, la:la + 1, :].astype(jnp.float32)
 
     barrier = pltpu.get_barrier_semaphore()
@@ -297,7 +356,12 @@
         return pltpu.make_async_remote_copy(src, dst, send_sem.at[SID[key]], recv_sem.at[SID[key]], device_id=dev, device_id_type=MESH)
 
     def same_size(key):
-        piece = rs.at[0, 0] if key[0] == 'R' else full.at[0, 0, pl.ds(0, KROWS[key]), :]
+        if key[0] == 'R':
+            piece = rs.at[0, 0]
+        elif key[0] == 'S':
+            piece = st_in.at[key[2]]
+        else:
+            piece = full.at[0, 0, pl.ds(0, KROWS[key]), pl.ds(0, width(key))]
         return remote(key, piece, piece, dev_p)
 
     def arrived(key):
@@ -308,10 +372,12 @@
         if i >= W_ITEM:
             if i == W_ITEM + 2:
                 return [(wd.at[la, pl.ds(3 * BLK, BLK), :], 0, D)]
-            cols = [1024 * (4 * (i - W_ITEM) + n) + 3 * BLK for n in range(4)]
+            cols = [1024 * (4 * (i - W_ITEM) + n) + 3 * BLK for n in QUAD]
         elif i in H_ITEMS:
             j = i - ATTN0[la] - 4
-            cols = [m256(4096 * (n // 2) + 2048 * side + 1024 * (n % 2) + BLK * j) for n in range(4)]
+            cols = [m256(shared_col(n, side, j)) for n in QUAD]
+        elif ITEMS[i] == 'Q':
+            return [((wq, wk, wv)[i].at[0, :, pl.ds(m256(HALF * side), HALF)], 0, HALF)]
         else:
             return [((wq, wk, wv, wo)[i - ATTN0[la]].at[la], 0, D)]
         out = []
@@ -327,7 +393,7 @@
             remote(key, src.at[part, :], full.at[i, me, part, pl.ds(c0, nc)], dev).start()
 
     def push(key, blk, off, dev):
-        piece = full.at[key[1], blk, pl.ds(off, KROWS[key]), :]
+        piece = full.at[key[1], blk, pl.ds(off, KROWS[key]), pl.ds(0, width(key))]
         remote(key, piece, piece, dev).start()
 
     def push_n(key, off, dev):
@@ -348,6 +414,13 @@
         if op[0] == 'drain':
             return same_size(key).wait_send()
         kind = key[0]
+        if kind == 'T':
+            return remote(key, x_hbm.at[pl.ds(key[2] * SEQ, SEQ), :], xo.at[key[2]], dev_x).start()
+        if kind == 'S':
+            return remote(key, st_out.at[key[2]], st_in.at[key[2]], dev_x).start()
+        if kind == 'O':
+            sq = pl.ds(key[2] * SEQ, SEQ)
+            return remote(key, act.at[1, sq, pl.ds(HALF, HALF)], act.at[4, sq, pl.ds(m256(HALF * xx), HALF)], dev_x).start()
         if kind == 'H':
             la, s = key[1:]
             return remote(key, h2.at[la, s, pl.ds(0, SEQ), :], h2.at[la, s, pl.ds(SEQ, SEQ), :], dev_x).start()
@@ -383,17 +456,17 @@
             pltpu.make_async_copy(src, dst, wt_sem.at[slot]).start()
 
     def others(i, n):
-        slot = n % 2
+        slot = n % SLOTS
         cols = pl.ds(n * TILE, TILE)
         load([(full.at[i, (me + k) % N_BLK, :, cols], wt.at[slot, (me + k) % N_BLK]) for k in range(1, N_BLK)], slot)
 
     def wait_tile(n, blocks=N_BLK):
-        slot = n % 2
+        slot = n % SLOTS
         part = wt.at[slot, pl.ds(0, blocks)]
         pltpu.make_async_copy(full.at[0, pl.ds(0, blocks), :, pl.ds(0, TILE)], part, wt_sem.at[slot]).wait()
 
     def load_mm(i, la, role, n):
-        slot = n % 2
+        slot = n % SLOTS
         cols = pl.ds(n * TILE, TILE)
         for k, w in enumerate((wq, wk, wv, wo)):
             pl.when(role == k)(functools.partial(load, [(w.at[la, :, cols], wt.at[slot, me])], slot))
@@ -401,13 +474,13 @@
         others(i, n)
 
     def load_gu(i, la, col, n):
-        slot = n % 2
+        slot = n % SLOTS
         c = pl.ds(m256(col(n)), BLK)
         load([(wg.at[la, :, c], wt.at[slot, me, :, pl.ds(0, BLK)]), (wu.at[la, :, c], wt.at[slot, me, :, pl.ds(BLK, BLK)])], slot)
         others(i, n)
 
     def load_dn(hn, la, j, n):
-        slot = n % 2
+        slot = n % SLOTS
         cols = pl.ds(n * TILE, TILE)
         parts = [(wd.at[la, pl.ds(m256(j * BLK), BLK), cols], wt.at[slot, n_me])]
         parts += [(full_n.at[hn, (n_me + k) % 4, :, cols], wt.at[slot, (n_me + k) % 4]) for k in range(1, 4)]
@@ -426,7 +499,7 @@
             body(pl.multiple_of(r * RB, RB))
             return carry
 
-        lax.fori_loop(0, SEQ // RB, step, 0)
+        loop(SEQ // RB, step)
 
     def act_rows(s, r0):
         return pl.ds(pl.multiple_of(s * SEQ + r0, RB), RB)
@@ -439,45 +512,49 @@
             c = cos_ref[pl.ds(r0, RB), :]
             sn = sin_ref[pl.ds(r0, RB), :]
             for h in range(D // HEAD_DIM):
-                part = v[:, h * HEAD_DIM:(h + 1) * HEAD_DIM]
+                part = v[:, head(h)]
                 turned = pltpu.roll(part, HEAD_DIM // 2, 1)
-                act[dst, act_rows(s, r0), h * HEAD_DIM:(h + 1) * HEAD_DIM] = (part * c + turned * sn).astype(jnp.bfloat16)
+                act[dst, act_rows(s, r0), head(h)] = (part * c + turned * sn).astype(jnp.bfloat16)
 
         rows(body)
 
-    def attention(q8, s):
+    def attention(q8, la, s):
+        split = (la == 0) & (q8 == 0)
+        dst = jnp.where(split, 4, 1)
+        base = jnp.where(split, xx * (HALF), q8 * (HALF))
         row = lax.broadcasted_iota(jnp.int32, (SEQ, SEQ), 0)
         col = lax.broadcasted_iota(jnp.int32, (SEQ, SEQ), 1)
         causal = row >= col
-        sq = pl.ds(pl.multiple_of(s * SEQ, SEQ), SEQ)
+        sq = seq(s)
 
         def step(h, carry):
-            for u in range(2):
+            for u in PAIRED:
                 lanes = pl.ds(pl.multiple_of((q8 * 8 + h * 2 + u) * HEAD_DIM, HEAD_DIM), HEAD_DIM)
                 q, k, v = act[1, sq, lanes], act[2, sq, lanes], act[3, sq, lanes]
                 sc = lax.dot_general(q, k, (((1,), (1,)), ((), ())), preferred_element_type=jnp.float32) * (HEAD_DIM ** -0.5)
                 sc = jnp.where(causal, sc, -jnp.inf)
                 e = jnp.exp(sc - jnp.max(sc, axis=-1, keepdims=True))
                 p = (e / jnp.sum(e, axis=-1, keepdims=True)).astype(jnp.bfloat16)
-                act[1, sq, lanes] = jnp.dot(p, v, preferred_element_type=jnp.float32).astype(jnp.bfloat16)
+                out = pl.ds(pl.multiple_of(base + (h * 2 + u) * HEAD_DIM, HEAD_DIM), HEAD_DIM)
+                act[dst, sq, out] = jnp.dot(p, v, preferred_element_type=jnp.float32).astype(jnp.bfloat16)
             return carry
 
-        lax.fori_loop(0, 4, step, 0)
+        loop(4, step)
 
     def mm(i, la, role, hf):
         s0 = jnp.where(hf == 2, 0, hf)
         s1 = jnp.where(hf == 2, 2, hf + 1)
-        lhs = jnp.where(role < 3, 0, jnp.where(role == 3, 1, 4))
+        lhs = jnp.where(role < 3, 0, jnp.where((role == 3) & (la == 1), 1, 4))
         load_mm(i, la, role, 0)
         for n in range(N_TILE):
             if n + 1 < N_TILE:
                 load_mm(i, la, role, n + 1)
             wait_tile(n)
-            cols = slice(n * TILE, (n + 1) * TILE)
+            cols = tile(n)
 
             def one(s, carry):
-                left = act[lhs, pl.ds(pl.multiple_of(s * SEQ, SEQ), SEQ), :]
-                prod = jnp.dot(left, wt[n % 2].reshape(D, TILE), preferred_element_type=jnp.float32)
+                left = act[lhs, seq(s), :]
+                prod = jnp.dot(left, wt[n % SLOTS].reshape(D, TILE), preferred_element_type=jnp.float32)
                 acc[s, :SEQ, cols] = jnp.where(role == 4, acc[s, :SEQ, cols], 0.0) + prod
                 return carry
 
@@ -513,17 +590,91 @@
 
         lax.fori_loop(s0, s1, epilogue, 0)
 
+    def load_mq(k, n):
+        slot = n % SLOTS
+        for r, w in enumerate((wq, wk, wv)):
+            own = w.at[0, :, pl.ds(m256(HALF * xx + n * TILE), TILE)]
+            pl.when(k == r)(functools.partial(load, [(own, wt.at[slot, me])], slot))
+        others(k, n)
+
+    def shared_qkv(k):
+        load_mq(k, 0)
+        for n in PAIRED:
+            if n == 0:
+                load_mq(k, 1)
+            wait_tile(n)
+            cols = tile(n)
+
+            def one(s, carry):
+                w = wt[n % SLOTS].reshape(D, TILE)
+                sq = seq(s)
+                acc[s, :SEQ, cols] = jnp.dot(act[0, sq, :], w, preferred_element_type=jnp.float32)
+                acc[s, SEQ:, cols] = jnp.dot(xo[s], w, preferred_element_type=jnp.float32)
+                return carry
+
+            loop(2, one)
+
+        @pl.when(k == 2)
+        def _():
+            def keep(s, carry):
+                for part in PAIRED:
+                    def body(r0, part=part):
+                        v = acc[s, pl.ds(part * SEQ + r0, RB), :HALF]
+                        act[3, act_rows(s, r0), part * (HALF):(part + 1) * (HALF)] = v.astype(jnp.bfloat16)
+
+                    rows(body)
+                return carry
+
+            loop(2, keep)
+
+        @pl.when(k < 2)
+        def _():
+            def squares(s, carry):
+                for part in PAIRED:
+                    for r in PAIRED:
+                        r0 = part * SEQ + r * HEAD_DIM
+                        total = jnp.zeros((HEAD_DIM, HEAD_DIM), jnp.float32)
+                        for h in range(8):
+                            a = acc[s, r0:r0 + HEAD_DIM, head(h)].astype(jnp.bfloat16).astype(jnp.float32)
+                            total = total + a * a
+                        col = jnp.broadcast_to(jnp.sum(total, axis=-1, keepdims=True), (HEAD_DIM, HEAD_DIM))
+                        st_out[k, s * 2 + part, :, head(r)] = col.T[:8, :]
+                return carry
+
+            loop(2, squares)
+
+    def shared_rope(k):
+        gain = jnp.concatenate([gains[xx * 4 + f, pl.ds(k, 1), :] for f in QUAD], axis=1)
+
+        def one(s, carry):
+            for part in PAIRED:
+                for r in PAIRED:
+                    lanes = head(r)
+                    sums = st_out[k, s * 2 + part, :, lanes] + st_in[k, s * 2 + 1 - part, :, lanes]
+                    col = jnp.broadcast_to(sums[:1, :], (HEAD_DIM, HEAD_DIM)).T
+                    inv = lax.rsqrt(col * (1.0 / D) + EPS)
+                    c, sn = cos_ref[lanes, :], sin_ref[lanes, :]
+                    r0 = part * SEQ + r * HEAD_DIM
+                    rr = pl.ds(pl.multiple_of(s * SEQ + r * HEAD_DIM, HEAD_DIM), HEAD_DIM)
+                    for h in range(8):
+                        hs = head(h)
+                        a = acc[s, r0:r0 + HEAD_DIM, hs].astype(jnp.bfloat16).astype(jnp.float32)
+                        v = a * inv * gain[:, hs]
+                        turned = pltpu.roll(v, HEAD_DIM // 2, 1)
+                        o0 = part * (HALF) + h * HEAD_DIM
+                        act[k + 1, rr, o0:o0 + HEAD_DIM] = (v * c + turned * sn).astype(jnp.bfloat16)
+            return carry
+
+        loop(2, one)
+
     def swiglu(prod):
         gate = prod[:, :BLK].astype(jnp.bfloat16).astype(jnp.float32)
         up = prod[:, BLK:].astype(jnp.bfloat16).astype(jnp.float32)
         return (jax.nn.silu(gate) * up).astype(jnp.bfloat16)
 
-    def halves(hf):
-        return jnp.where(hf == 2, 0, hf), jnp.where(hf == 2, 2, hf + 1)
-
     def shared_mlp(i, hn, la, j, s):
         def col(n):
-            return 4096 * (n // 2) + 2048 * xx + 1024 * (n % 2) + BLK * j
+            return shared_col(n, xx, j)
 
         load_gu(i, la, col, 0)
         for n in range(N_TILE):
@@ -532,14 +683,14 @@
             else:
                 load_dn(hn, la, j, 0)
             wait_tile(n)
-            prod = jnp.dot(h2[la, s], wt[n % 2].reshape(D, TILE), preferred_element_type=jnp.float32)
+            prod = jnp.dot(h2[la, s], wt[n % SLOTS].reshape(D, TILE), preferred_element_type=jnp.float32)
             mj[:, n * BLK:(n + 1) * BLK] = swiglu(prod)
         for n in range(N_TILE):
             if n + 1 < N_TILE:
                 load_dn(hn, la, j, n + 1)
             wait_tile(n, 4)
-            cols = slice(n * TILE, (n + 1) * TILE)
-            prod = jnp.dot(mj[...], wt[n % 2, :4].reshape(4 * BLK, TILE), preferred_element_type=jnp.float32)
+            cols = tile(n)
+            prod = jnp.dot(mj[...], wt[n % SLOTS, :4].reshape(4 * BLK, TILE), preferred_element_type=jnp.float32)
             acc[s, :, cols] = jnp.where(j > 0, acc[s, :, cols], 0.0) + prod
 
     def plain_gu(i, e):
@@ -553,11 +704,11 @@
             wait_tile(n)
 
             def one(s, carry):
-                prod = jnp.dot(h2[1, s, :SEQ], wt[n % 2].reshape(D, TILE), preferred_element_type=jnp.float32)
-                act[4, pl.ds(pl.multiple_of(s * SEQ, SEQ), SEQ), pl.ds(m256(e * 1024 + n * BLK), BLK)] = swiglu(prod)
+                prod = jnp.dot(h2[1, s, :SEQ], wt[n % SLOTS].reshape(D, TILE), preferred_element_type=jnp.float32)
+                act[4, seq(s), pl.ds(m256(e * 1024 + n * BLK), BLK)] = swiglu(prod)
                 return carry
 
-            lax.fori_loop(0, 2, one, 0)
+            loop(2, one)
 
     def finish(la, s):
         gain = gain_row(la, 3)
@@ -580,7 +731,7 @@
         cp = pltpu.make_async_remote_copy(gain_ref, gains.at[me], gs_sem.at[k], gr_sem.at[k], device_id=(zz, (me + k) % N_BLK), device_id_type=MESH)
         gain_copies.append(cp)
 
-    types = ['mm', 'at', 'h', 'wgu', 'wd', 'fin']
+    types = ['mm', 'at', 'h', 'wgu', 'wd', 'fin', 'mq', 'nr']
 
     def step(p, carry):
         for k in range(n_slot):
@@ -607,13 +758,15 @@
         hf = pick(p, [o[4] for o in order])
         hn = pick(p, [H_ITEMS.index(o[1]) if o[0] == 'h' else 0 for o in order])
         pl.when((ty == 0) | (ty == 4))(lambda: mm(item, la, ex, hf))
-        pl.when(ty == 1)(lambda: attention(ex, hf))
+        pl.when(ty == 1)(lambda: attention(ex, la, hf))
         pl.when(ty == 2)(lambda: shared_mlp(item, hn, la, ex, hf))
         pl.when(ty == 3)(lambda: plain_gu(item, ex))
         pl.when(ty == 5)(lambda: finish(la, hf))
+        pl.when(ty == 6)(lambda: shared_qkv(ex))
+        pl.when(ty == 7)(lambda: shared_rope(ex))
         return carry
 
-    lax.fori_loop(0, n_slot, step, 0)
+    loop(n_slot, step)
 
     out_copy = pltpu.make_async_copy(act.at[0], out_hbm, io_sem)
     out_copy.start()
@@ -647,6 +800,9 @@
                 pltpu.VMEM((2 * SEQ, 4 * BLK), jnp.bfloat16),
                 pltpu.VMEM((2, 2 * SEQ, D), jnp.float32),
                 pltpu.VMEM((2, 2, SEQ, D), jnp.float32),
+                pltpu.VMEM((2, SEQ, D), jnp.bfloat16),
+                pltpu.VMEM((2, 4, 8, SEQ), jnp.float32),
+                pltpu.VMEM((2, 4, 8, SEQ), jnp.float32),
                 pltpu.VMEM((2, N_BLK, BLK, TILE), jnp.bfloat16),
                 pltpu.VMEM((N_BLK, 8, BLK), jnp.float32),
                 pltpu.VMEM((4, 2, BLK), jnp.bfloat16),

time: 595 us -> 589 us (0.990)
  Pallas kernels: 589 us -> 583 us
where the time goes in v4:
time: 589 us; the launch traced here: 586 us
  Pallas kernels  583 us (99%)
    pallas_call x1, Pallas kernels, local_fn(): pl.pallas_call(kernel, out_shape=(jax.ShapeDtypeStruct((ROWS, D), jnp.bfl...  583 us

profile of v4, /device:TPU:0, one launch (start us, length us, event | category | flops | bytes accessed | tf_op | source)
XLA Modules:
  0.0 586.5 jit_solution(5507536699246778757)
XLA Ops:
  0.0 583.3 %shard_map.136 = (bf16[512,2048]{1,0:T(8,128)(2,1)}, bf16[18,8,256,2048]{3,2,1,0:T(8,128)(2,1)}, bf16[7,4,256,2048]{3,2,1,0:T(8,128)(2,1)}) custom-call(bf16[512,2048]{1,0:T(8,128)(2,1)} %bitcast.2, f32[256,128]{1,0:T(8,128)} %constant.4.clone.cos_ref, f32[256,128]{1,0:T(8,128)} %constant.5.clone.sin_ref, bf16[2,256]{1,0:T(2,128)(2,1)} %gq.1, ...), custom_call_target="tpu_custom_call" | custom-call | tf_op jit(solution)/shard_map/pallas_call | solution.py:788
  583.3 3.2 copy.16

commit v5 on v4

--- a/solution.py
+++ b/solution.py
@@ -31,12 +31,12 @@
 UNIT = ONE_MIB / 256
 LAT = 2.5
 PAIR = 4.0
-FLOW = {'A': (176, 144, 64), 'B': (144, 176, 144), 'C': (144, 176, 144), 'Q': (128, 128, 128), 'H': (144, 128, 128), 'G': (176, 144, 144)}
-VIA_X = {'A': 64}
-DOWN = {'H': 176, 'G': 208}
+FLOW = {'A': (176, 128, 16), 'B': (144, 160, 128), 'C': (144, 176, 128), 'Q': (144, 128, 128), 'H': (176, 128, 128), 'G': (128, 192, 128)}
+VIA_X = {'A': 112}
+DOWN = {'H': 160, 'G': 208}
 FLOW = {k: (px, py, VIA_X.get(k, 0), dy, DOWN.get(k, 0)) for k, (px, py, dy) in FLOW.items()}
 ITEMS = ['Q'] * 3 + ['A'] + ['H'] * 4 + ['B'] * 4 + ['G'] * 3 + ['C'] * 3
-BACKLOG = 8.0
+BACKLOG = 10.0
 N_H = (4, 3)
 COST = {'mm': 6.6, 'at': 4.5, 'h': 10.5, 'wgu': 7.5, 'wd': 11.0, 'fin': 1.5}
 SCALE = {'Q': 0.5}
@@ -121,7 +121,7 @@
             add('ZN', 'z', (BLK - pn) * UNIT, 'N')
             add('Q1', 'p', PAIR, 'N', 'ZN')
     for h in PAIRED:
-        todo_send[('T', 0, h)] = (-2, 'x', ONE_MIB, [])
+        todo_send[('T', 0, h)] = (0.5, 'x', ONE_MIB, [])
     limit = dict(x=thr, y=thr, z=thr, p=2 * PAIR)
 
     def needs(s):

time: 589 us -> 587 us (level)
  no operation moved by 1% of the time
where the time goes in v5:
time: 587 us; the launch traced here: 585 us
  Pallas kernels  582 us (99%)
    pallas_call x1, Pallas kernels, local_fn(): pl.pallas_call(kernel, out_shape=(jax.ShapeDtypeStruct((ROWS, D), jnp.bfl...  582 us

profile of v5, /device:TPU:0, one launch (start us, length us, event | category | flops | bytes accessed | tf_op | source)
XLA Modules:
  0.0 584.8 jit_solution(13014392393825447349)
XLA Ops:
  0.0 581.6 %shard_map.136 = (bf16[512,2048]{1,0:T(8,128)(2,1)}, bf16[18,8,256,2048]{3,2,1,0:T(8,128)(2,1)}, bf16[7,4,256,2048]{3,2,1,0:T(8,128)(2,1)}) custom-call(bf16[512,2048]{1,0:T(8,128)(2,1)} %bitcast.2, f32[256,128]{1,0:T(8,128)} %constant.4.clone.cos_ref, f32[256,128]{1,0:T(8,128)} %constant.5.clone.sin_ref, bf16[2,256]{1,0:T(2,128)(2,1)} %gq.1, ...), custom_call_target="tpu_custom_call" | custom-call | tf_op jit(solution)/shard_map/pallas_call | solution.py:788
  581.6 3.2 copy.16
